TPU v7x, 512 devices: a whole 4x8x8 slice. The times are simulated.
512 devices in a mesh: sys: 32 (over z, y_hi), mode: 8 (over y_lo, x), rank: 2 (over core).
Axes of the slice: x: 4, y: 8 (y_hi: 4, y_lo: 2; y = y_hi * 2 + y_lo), z: 8, core: 2. Of those that a mesh axis runs over, the one named last changes fastest.
Arguments:
- solution_core: bfloat16 [2048, 256, 64], P(('sys', 'rank'), 'mode'), parts along dimension 0, may hold values from -6 to 6
- operator_core: bfloat16 [256, 256, 256, 8], P('sys', 'rank', 'mode'), parts along dimension 0, may hold values from -0.125 to 0.125
- left_interface: bfloat16 [2048, 8, 64], P('sys', None, 'rank'), parts along dimension 0, may hold values from -0.25 to 0.25
- right_interface: bfloat16 [2048, 8, 16], P('sys'), parts along dimension 0, may hold values from -0.75 to 0.75
- rhs_left: bfloat16 [2048, 16], P(('sys', 'rank')), parts along dimension 0, may hold values from -1.5 to 1.5
- rhs_core: bfloat16 [512, 256, 16], P('sys', 'mode'), parts along dimension 0, may hold values from -6 to 6
- rhs_right: bfloat16 [512, 16], P('sys'), parts along dimension 0, may hold values from -1.5 to 1.5
Outputs:
- q_core: float32 [2048, 256, 80], P(('sys', 'rank'), 'mode'), parts along dimension 0
- r_factor: float32 [2560, 80], P('sys'), parts along dimension 0
There are 32 independent parts, one for each index of `sys`. A program takes and returns all parts, laid end to end along the dimension named above; each array names one. Nothing has to cross between parts.
All inputs are finite; a program needn't handle non-finite values.
Results may differ from a plain program's by a relative error of at most 0.0014.
Values may be sent and summed in bfloat16 or wider, within the bound.
No kernel may reach another device: no remote copies, remote signals or barrier semaphores. Data moves between devices by JAX's collectives and lax.ppermute only.
A program may use at most 64 MiB of HBM per device.

v0:
```python
import jax
import jax.numpy as jnp
from jax import lax
from jax.sharding import PartitionSpec as P


def side_by_side(arrays, axis, dim, along):
    columns = [a.reshape(*a.shape[:along], -1) for a in arrays]
    both = jnp.concatenate(columns, axis=along)
    out, at, done = (lax.all_gather(both, axis, axis=dim, tiled=True), 0, [])
    for a, column in zip(arrays, columns):
        piece = out[..., at : at + column.shape[along]]
        done.append(piece.reshape(*piece.shape[:along], *a.shape[along:]))
        at += column.shape[along]
    return tuple(done)


def in_blocks(value, dim, length):
    before, after = (value.shape[:dim], value.shape[dim + 1 :])
    return jnp.moveaxis(value.reshape(*before, length, -1, *after), dim, 0)


def sum_at_owner(value, axis, dim):
    parts = in_blocks(value, dim, lax.axis_size(axis))
    arrived = lax.all_to_all(parts, axis, split_axis=0, concat_axis=0, tiled=True)
    return arrived.sum(axis=0)


def from_everyone(value, axis):
    length = lax.axis_size(axis)
    return lax.all_to_all(
        jnp.broadcast_to(value[None], (length, *value.shape)), axis, 0, 0, tiled=True
    )


def taken_together(value, axis):
    everything = from_everyone(value, axis)
    return jnp.sum(everything, axis=0)


def per_device(
    solution_core, operator_core, left_interface, right_interface, rhs_left, rhs_core, rhs_right
):
    f32 = jnp.float32
    highest = lax.Precision.HIGHEST
    left_rows, mode_rows, rank_full = solution_core.shape
    resid_rank = right_interface.shape[2]
    core_flat = solution_core.astype(f32).reshape(left_rows * mode_rows, rank_full)
    projected = jnp.einsum(
        "cjd,dyb->cjyb", solution_core, right_interface, preferred_element_type=f32
    ).astype(jnp.bfloat16)
    inter_turned = jnp.transpose(left_interface, (2, 1, 0))
    proj_piece, inter_piece = side_by_side((projected, inter_turned), "rank", 0, 1)
    applied = jnp.einsum(
        "xijy,cjyb->cxib", operator_core, proj_piece, preferred_element_type=f32
    ).astype(jnp.bfloat16)
    partial_value = jnp.einsum("cxa,cxib->aib", inter_piece, applied, preferred_element_type=f32)
    turned = lax.all_to_all(partial_value, "rank", split_axis=0, concat_axis=1, tiled=True)
    summed = sum_at_owner(turned, "mode", 1)
    rhs_term = jnp.einsum(
        "af,fig,gb->aib",
        rhs_left.astype(f32),
        rhs_core.astype(f32),
        rhs_right.astype(f32),
        precision=highest,
    )
    residual_core = rhs_term - summed
    resid_flat = residual_core.reshape(left_rows * mode_rows, resid_rank)
    enriched = jnp.concatenate([core_flat, resid_flat], axis=1)
    gram = taken_together(jnp.dot(enriched.T, enriched, precision=highest), ("mode", "rank"))
    lower = jnp.linalg.cholesky(gram)
    solved = lax.linalg.triangular_solve(
        lower, enriched, left_side=False, lower=True, transpose_a=True
    )
    q_core = solved.reshape(left_rows, mode_rows, rank_full + resid_rank)
    return (q_core, lower.T)


def solution(mesh):
    in_specs = (
        P(("sys", "rank"), "mode", None),
        P("sys", "rank", "mode", None),
        P("sys", None, "rank"),
        P("sys", None, None),
        P(("sys", "rank"), None),
        P("sys", "mode", None),
        P("sys", None),
    )
    out_specs = (P(("sys", "rank"), "mode", None), P("sys", None))
    return jax.shard_map(
        per_device, mesh=mesh, in_specs=in_specs, out_specs=out_specs, check_vma=False
    )
```

profile of v0, /device:TPU:1, one launch (start us, length us, event | category | flops | bytes accessed | tf_op | source)
XLA Modules:
  0.0 79.8 jit_solution(8435781105677740832)
XLA Ops:
  0.7 1.6 %convolution_convert_fusion = bf16[32,32,8,16]{1,3,2,0:T(8,128)(2,1)S(1)} fusion(bf16[32,32,64]{2,1,0:T(8,128)(2,1)} %param.7, bf16[64,8,16]{0,2,1:T(8,128)(2,1)} %param.10), kind=kOutput, calls=%fused_computation.3 | convolution fusion | flops 16908288 | bytes 409600 | tf_op jit(solution)/shard_map/cjd,dyb->cjyb/dot_general | solution.py:49
  2.2 2.2 %copy.61 = bf16[32,32,8,16]{0,3,2,1:T(8,128)(2,1)S(1)} copy(bf16[32,32,8,16]{1,3,2,0:T(8,128)(2,1)S(1)} %convolution_convert_fusion) | data formatting | bytes 524288 | tf_op jit(solution)/shard_map/convert_element_type | solution.py:51
  5.0 8.7 %all_gather.3 = bf16[64,4608]{1,0:T(8,128)(2,1)S(1)} all-gather(bf16[32,4608]{1,0:T(8,128)(2,1)S(1)} %pad_maximum_fusion), channel_id=1, replica_groups=mesh['sys'=32,'mode'=8,'rank'=2] {'rank'}, dimensions={0}, use_global_device_ids=true | all-gather | bytes 884736 | tf_op jit(solution)/shard_map/all_gather | solution.py:10
  13.7 0.5 copy.91
  14.3 1.1 %fusion.2 = f32[64,128,16]{1,0,2:T(8,128)S(1)} fusion(bf16[64,8,64,1]{0,2,1,3:T(8,128)(2,1)S(1)} %bitcast.84, bf16[64,32,8,16,1]{0,3,2,1,4:T(8,128)(2,1)S(1)} %bitcast.81, bf16[8,128,32,8]{1,3,2,0:T(8,128)(2,1)S(1)} %copy-done), kind=kOutput, calls=%fused_computation.4 | convolution fusion | flops 672137216 | bytes 1638400 | tf_op jit(solution)/shard_map/cxa,cxib->aib/dot_general | solution.py:57
  15.8 4.2 %all_to_all.25 = f32[64,128,16]{1,2,0:T(8,128)S(1)} all-to-all(f32[64,128,16]{1,2,0:T(8,128)S(1)} %copy.67), channel_id=1, replica_groups=mesh['sys'=32,'mode'=8,'rank'=2] {'rank'}, dimensions={0} | all-to-all | bytes 1048576 | tf_op jit(solution)/shard_map/all_to_all | solution.py:58
  20.3 0.8 %reshape.46 = f32[32,8,32,16]{2,1,3,0:T(8,128)S(1)} reshape(f32[32,2,128,16]{2,1,3,0:T(2,128)S(1)} %bitcast.82) | data formatting | bytes 1048576 | tf_op jit(solution)/shard_map/reshape | solution.py:20
  21.1 1.7 %copy.100 = f32[8,32,32,16]{2,3,1,0:T(8,128)} copy(f32[8,32,32,16]{2,0,3,1:T(8,128)S(1)} %bitcast.76) | data formatting | bytes 1048576 | tf_op jit(solution)/shard_map/transpose | solution.py:20
  22.9 3.1 %reshape.59 = f32[8,1,16384]{2,1,0:T(1,128)} reshape(f32[8,32,16,32]{3,2,1,0:T(8,128)} %bitcast.77) | data formatting | bytes 1048576
  26.0 3.5 %all-to-all-start.1 = ((f32[8,1,16384]{2,1,0:T(1,128)}), f32[8,1,16384]{2,1,0:T(1,128)S(1)}, u32[]{:S(2)}, u32[]{:S(2)}) async-start(f32[8,1,16384]{2,1,0:T(1,128)} %reshape.59), calls=%async_computation.1 | async-start | bytes 1048576 | tf_op jit(solution)/shard_map/all_to_all | solution.py:25
  29.8 8.1 %all-to-all-done.1 = f32[8,1,16384]{2,1,0:T(1,128)S(1)} async-done(((f32[8,1,16384]{2,1,0:T(1,128)}), f32[8,1,16384]{2,1,0:T(1,128)S(1)}, u32[]{:S(2)}, u32[]{:S(2)}) %all-to-all-start.1) | async-done | bytes 524320 | tf_op jit(solution)/shard_map/all_to_all | solution.py:25
  37.9 0.5 broadcast.48
  38.4 2.8 %reduce.6 = f32[8,16384]{1,0:T(8,128)} reduce(f32[8,1,16384]{2,1,0:T(1,128)S(1)} %all-to-all-done.1, f32[]{:T(128)} %broadcast.48), dimensions={1}, to_apply=%all_to_all.20.reduce_sub_computation | reduce | bytes 1048580 | tf_op jit(solution)/shard_map/all_to_all | solution.py:25
  41.2 1.7 %reshape.60 = f32[8,32,16,32]{3,2,1,0:T(8,128)S(1)} reshape(f32[8,16384]{1,0:T(8,128)} %reduce.6) | data formatting | bytes 1048576
  43.7 0.4 fusion.5
  44.1 0.5 copy.72
  44.6 1.3 %fusion.12 = f32[80,80]{1,0:T(8,128)S(1)} fusion(f32[1024,16]{1,0:T(8,128)S(1)} %bitcast.79, f32[1024,64]{1,0:T(8,128)S(1)} %bitcast.78), kind=kOutput, calls=%fused_computation.12 | convolution fusion | flops 78725120 | bytes 353280 | tf_op jit(solution)/shard_map/dot_general | solution.py:70
  46.0 16.8 %all_to_all.26 = f32[16,80,80]{2,1,0:T(8,128)S(1)} all-to-all(f32[16,80,80]{2,1,0:T(8,128)S(1)} %broadcast_in_dim.3), channel_id=1, replica_groups=mesh['sys'=32,'mode'=8,'rank'=2] {'mode','rank'}, dimensions={0} | all-to-all | bytes 819200 | tf_op jit(solution)/shard_map/all_to_all | solution.py:31
  62.9 7.3 %cholesky.16 = f32[80,80]{1,0:T(8,128)S(1)} custom-call(f32[80,80]{1,0:T(8,128)S(1)} %fusion.21), custom_call_target="Cholesky" | custom-call | tf_op jit(solution)/shard_map/jit(cholesky)/cholesky | solution.py:71
  70.3 0.6 compare_reduce_fusion
  70.9 0.7 fusion.22
  71.6 6.1 %custom-call.6 = f32[1,80,80]{1,2,0:T(8,128)S(1)} custom-call(f32[1,80,80]{2,1,0:T(8,128)S(1)} %get-tuple-element.13), custom_call_target="InvertDiagBlocksLowerTriangular" | custom-call | tf_op jit(solution)/shard_map/triangular_solve | solution.py:72
  77.7 1.4 %fusion.8 = f32[32,32,80]{2,1,0:T(8,128)} fusion(f32[32,32,16]{2,1,0:T(8,128)S(1)} %copy.72, f32[32,32,64]{2,1,0:T(8,128)S(1)} %convert_element_type.15, f32[1,80,80]{1,2,0:T(8,128)S(1)} %custom-call.6), kind=kOutput, calls=%fused_computation.8 | convolution fusion | flops 78725120 | bytes 680960 | tf_op jit(solution)/shard_map/triangular_solve | solution.py:72
  79.1 0.7 copy.77
  (30 shorter events, 2.5 us)
Async XLA Ops:
  0.6 13.7 %copy-start = (bf16[8,128,32,8]{1,3,2,0:T(8,128)(2,1)S(1)}, bf16[8,128,32,8]{1,3,2,0:T(8,128)(2,1)}, u32[]{:S(2)}) copy-start(bf16[8,128,32,8]{1,3,2,0:T(8,128)(2,1)} %param.8) | copy-start | bytes 1572868
  0.6 4.1 %copy-start.3 = (bf16[64,8,32]{0,2,1:T(8,128)(2,1)S(1)}, bf16[64,8,32]{0,2,1:T(8,128)(2,1)}, u32[]{:S(2)}) copy-start(bf16[64,8,32]{0,2,1:T(8,128)(2,1)} %param.9) | copy-start | bytes 98308
  22.9 6.7 %copy-start.1 = (bf16[32,32,64]{2,1,0:T(8,128)(2,1)S(1)}, bf16[32,32,64]{2,1,0:T(8,128)(2,1)}, u32[]{:S(2)}) copy-start(bf16[32,32,64]{2,1,0:T(8,128)(2,1)} %param.7) | copy-start | bytes 393220
  22.9 6.7 %copy-start.2 = (bf16[16,32,16]{1,2,0:T(8,128)(2,1)S(1)}, bf16[16,32,16]{1,2,0:T(8,128)(2,1)}, u32[]{:S(2)}) copy-start(bf16[16,32,16]{1,2,0:T(8,128)(2,1)} %param.12) | copy-start | bytes 49156
  22.9 6.7 %copy-start.5 = (bf16[16,16]{1,0:T(8,128)(2,1)S(1)}, bf16[16,16]{1,0:T(8,128)(2,1)}, u32[]{:S(2)}) copy-start(bf16[16,16]{1,0:T(8,128)(2,1)} %param.13) | copy-start | bytes 1540
  26.0 11.9 %all-to-all-start.1 = ((f32[8,1,16384]{2,1,0:T(1,128)}), f32[8,1,16384]{2,1,0:T(1,128)S(1)}, u32[]{:S(2)}, u32[]{:S(2)}) async-start(f32[8,1,16384]{2,1,0:T(1,128)} %reshape.59), calls=%async_computation.1 | async-start | bytes 1048576 | tf_op jit(solution)/shard_map/all_to_all | solution.py:25
  43.0 0.7 copy-start.4
where the time goes:
time: 80.3 us; the launch traced here: 79.8 us
  blocking collectives  29.7 us (37%)
  other arithmetic  17.9 us (22%)
  local copies, waits for them, and re-layouts  13.8 us (17%)
  waiting for transfers between devices  8.11 us (10%)
  matrix products  5.98 us (7%)
  starting transfers between devices  3.49 us (4%)
  between operations  0.88 us (1%)
    all_to_all x1, blocking collectives, from_everyone(): lax.all_to_all(jnp.broadcast_to(value[None], (length, *value.shape)), axi...  16.8 us
    all_gather x1, blocking collectives, side_by_side(): out, at, done = (lax.all_gather(both, axis, axis=dim, tiled=True), 0, [])  8.69 us
    all_to_all x1, waiting for transfers between devices, sum_at_owner(): lax.all_to_all(parts, axis, split_axis=0, concat_axis=0, tiled=True)  8.11 us
    another operation x3, other arithmetic, per_device(): lower = jnp.linalg.cholesky(gram)  7.98 us
    unnamed x16, local copies, waits for them, and re-layouts  6.45 us
    another operation x1, other arithmetic, per_device(): lax.linalg.triangular_solve(lower, enriched, left_side=False, lower=True,...  6.13 us
    all_to_all x1, blocking collectives, per_device(): lax.all_to_all(partial_value, 'rank', split_axis=0, concat_axis=1, tiled=...  4.15 us
    all_to_all x1, starting transfers between devices, sum_at_owner(): lax.all_to_all(parts, axis, split_axis=0, concat_axis=0, tiled=True)  3.49 us
  transfers between devices with their start and end apart: 1, of which 1 were waited for; matrix products, arithmetic and copies ran while one was open for 0% of the time, Pallas kernels for 0%

commit v1 on v0

v1 whole, which is shorter than its diff:
```python
import jax
import jax.numpy as jnp
from jax import lax
from jax.experimental import pallas as pl
from jax.experimental.pallas import tpu as pltpu
from jax.sharding import PartitionSpec as P

INTERPRET = False
F32 = jnp.float32
BF16 = jnp.bfloat16
HIGHEST = lax.Precision.HIGHEST

R = 64
RZ = 16
RA = 8
HALF = 32
ROWS = 1024
NT = (((1,), (1,)), ((), ()))
TN = (((0,), (0,)), ((), ()))


def call(body, outs, *args, scratch=(), flops=0, **kw):
    return pl.pallas_call(
        body,
        out_shape=outs,
        scratch_shapes=scratch,
        interpret=INTERPRET,
        cost_estimate=pl.CostEstimate(flops=flops, bytes_accessed=1 << 20, transcendentals=0),
        **kw,
    )(*args)


def three_parts(x):
    hi = x.astype(BF16)
    rest = x - hi.astype(F32)
    mid = rest.astype(BF16)
    return hi, mid, (rest - mid.astype(F32)).astype(BF16)


def project(both_ref, right_ref, proj_ref, left_ref, gram_ref, sol_ref):
    sol_ref[0:ROWS] = both_ref[0, 0:ROWS].astype(F32)
    sol_ref[ROWS : 2 * ROWS] = both_ref[1, 0:ROWS].astype(F32)
    right = right_ref[...]
    for j in range(32):
        rows = sol_ref[pl.ds(j, R, stride=32), :].astype(BF16)
        proj_ref[j] = lax.dot_general(right, rows, NT, preferred_element_type=F32).astype(BF16)
    for x in range(RA):
        for r in range(2):
            left_ref[x, HALF * r : HALF * (r + 1)] = both_ref[r, ROWS + HALF * x : ROWS + HALF * (x + 1)]
    gram = jnp.zeros((R, R), F32)
    for r in range(2):
        s = both_ref[r, 0:ROWS]
        gram = gram + lax.dot_general(s, s, TN, preferred_element_type=F32)
    for p, part in enumerate(three_parts(gram)):
        part = part.astype(F32)
        gram_ref[HALF * p : HALF * (p + 1)] = jnp.concatenate([part[:HALF], part[HALF:]], axis=1).astype(BF16)


def pack(part_ref, out_ref):
    for half in range(2):
        for g in range(4):
            four = [part_ref[4 * g + k, HALF * half : HALF * (half + 1), :].astype(F32) for k in range(4)]
            for q in range(4):
                piece = jnp.concatenate([x[:, 32 * q : 32 * (q + 1)] for x in four], axis=1)
                out_ref[half, q, HALF * g : HALF * (g + 1)] = piece.astype(BF16)


def residual(recv_ref, rhs_ref, sol_ref, turned_ref, send_ref, gram_ref, rows_ref):
    total = recv_ref[0].astype(F32)
    for m in range(1, 8):
        total = total + recv_ref[m].astype(F32)
    packed = total[128:160] + total[160:192] + total[192:224]
    gram_ref[0:HALF] = packed[:, 0:R]
    gram_ref[HALF:R] = packed[:, R:]
    resid = rhs_ref[...] - total[0:128]
    for k in range(4):
        shifted = resid if k == 0 else pltpu.roll(resid, 128 - 32 * k, 1)
        for g in range(4):
            b = 4 * g + k
            rows_ref[HALF * b : HALF * (b + 1)] = shifted[HALF * g : HALF * (g + 1)]
    for t in range(8):
        four = [rows_ref[pl.ds(4 * t + s, RZ, stride=32), :] for s in range(4)]
        turned_ref[:, 128 * t : 128 * (t + 1)] = jnp.concatenate([x[:, :32] for x in four], axis=1)
    turned = turned_ref[...]
    stacked = jnp.concatenate(three_parts(turned), axis=0)
    cross = jnp.dot(stacked, sol_ref[...], preferred_element_type=F32)
    cross = cross[0:16] + cross[16:32] + cross[32:48]
    own = lax.dot_general(turned, turned, NT, precision=HIGHEST, preferred_element_type=F32)
    row = jnp.concatenate([cross, own, jnp.zeros((RZ, 48), F32)], axis=1)
    for k in range(16):
        send_ref[k] = row


def eliminate(m, n):
    index = lax.broadcasted_iota(jnp.int32, (n, 1), 0)
    for k in range(n):
        row = m[k : k + 1]
        factor = jnp.where(index > k, m[:, k : k + 1] / m[k : k + 1, k : k + 1], 0.0)
        m = m - factor * row
    lane = lax.broadcasted_iota(jnp.int32, m.shape, 1)
    pivot = jnp.sum(jnp.where(lane == index, m, 0.0), axis=1, keepdims=True)
    return m * lax.rsqrt(pivot)


def first_block(gram_ref, sol_ref, turned_ref, both_ref, rows_ref):
    eye = (lax.broadcasted_iota(jnp.int32, (R, R), 0) == lax.broadcasted_iota(jnp.int32, (R, R), 1)).astype(F32)
    both = eliminate(jnp.concatenate([gram_ref[...], eye], axis=1), R)
    both_ref[...] = both
    inverse = both[:, R:]
    ortho = lax.dot_general(sol_ref[...].astype(F32), inverse, NT, precision=HIGHEST, preferred_element_type=F32)
    rows_ref[...] = jnp.concatenate([ortho, turned_ref[...].T], axis=1)


def last_block(recv_ref, both_ref, rows_ref, q_ref, r_ref):
    total = recv_ref[0]
    for k in range(1, 16):
        total = total + recv_ref[k]
    both = both_ref[...]
    cross = lax.dot_general(total[:, :R], both[:, R:], NT, precision=HIGHEST, preferred_element_type=F32)
    schur = total[:, R : R + RZ] - lax.dot_general(cross, cross, NT, precision=HIGHEST, preferred_element_type=F32)
    eye = (lax.broadcasted_iota(jnp.int32, (RZ, RZ), 0) == lax.broadcasted_iota(jnp.int32, (RZ, RZ), 1)).astype(F32)
    last = eliminate(jnp.concatenate([schur, eye], axis=1), RZ)
    inverse = last[:, RZ:]
    mixed = jnp.dot(inverse, cross, precision=HIGHEST, preferred_element_type=F32)
    eye = (lax.broadcasted_iota(jnp.int32, (R, R + RZ), 0) == lax.broadcasted_iota(jnp.int32, (R, R + RZ), 1)).astype(F32)
    weight = jnp.concatenate([eye, jnp.concatenate([-mixed, inverse], axis=1)], axis=0)
    q_ref[...] = lax.dot_general(rows_ref[...], weight, NT, precision=HIGHEST, preferred_element_type=F32)
    r_ref[0:R] = jnp.concatenate([both[:, :R], cross.T], axis=1)
    r_ref[R:] = jnp.concatenate([jnp.zeros((RZ, R), F32), last[:, :RZ]], axis=1)


def per_device(solution_core, operator_core, left_interface, right_interface, rhs_left, rhs_core, rhs_right):
    shape = jax.ShapeDtypeStruct
    sol = solution_core.reshape(ROWS, R)
    left = jnp.transpose(left_interface, (1, 2, 0)).reshape(RA * HALF, R)
    both = lax.all_gather(jnp.concatenate([sol, left], axis=0), "rank", axis=0)
    right = jnp.transpose(right_interface, (1, 2, 0)).reshape(RA * RZ, R)
    proj, left, early = call(
        project,
        (shape((32, 128, R), BF16), shape((RA, R, R), BF16), shape((96, 128), BF16)),
        both,
        right,
        scratch=[pltpu.VMEM((2 * ROWS, R), F32)],
        flops=1 << 26,
    )
    proj = jnp.transpose(proj.reshape(32, RA, RZ, R), (3, 0, 1, 2))
    left = jnp.transpose(left, (1, 0, 2))
    applied = jnp.einsum("xijy,cjyb->cxib", operator_core, proj, preferred_element_type=F32).astype(BF16)
    partial_value = jnp.einsum("cxa,cxib->aib", left, applied, preferred_element_type=F32)
    partial_value = jnp.transpose(partial_value, (2, 0, 1)).astype(BF16)
    packed = call(pack, shape((2, 4, 128, 128), BF16), partial_value, flops=1 << 24)
    everyone = lax.all_gather(packed, "rank", axis=0)
    mine = lax.dynamic_index_in_dim(everyone, lax.axis_index("rank"), axis=1, keepdims=False)
    send = jnp.concatenate(
        [mine.reshape(8, 128, 128), jnp.broadcast_to(early[None], (8, 96, 128))], axis=1
    )
    recv = lax.all_to_all(send, "mode", split_axis=0, concat_axis=0, tiled=True)
    rhs_term = jnp.einsum(
        "af,fig,gb->aib", rhs_left.astype(F32), rhs_core.astype(F32), rhs_right.astype(F32), precision=HIGHEST
    )
    rhs_term = jnp.transpose(rhs_term.reshape(HALF, 32, 4, 4), (2, 0, 3, 1)).reshape(128, 128)
    turned, send, gram = call(
        residual,
        (shape((RZ, ROWS), F32), shape((16, RZ, 128), F32), shape((R, R), F32)),
        recv,
        rhs_term,
        sol,
        scratch=[pltpu.VMEM((512, 128), F32)],
        flops=1 << 24,
    )
    recv = lax.all_to_all(send, ("mode", "rank"), split_axis=0, concat_axis=0, tiled=True)
    factor, rows = call(
        first_block,
        (shape((R, 2 * R), F32), shape((ROWS, R + RZ), F32)),
        gram,
        sol,
        turned,
        flops=1 << 32,
    )
    q_core, r_factor = call(
        last_block,
        (shape((ROWS, R + RZ), F32), shape((R + RZ, R + RZ), F32)),
        recv,
        factor,
        rows,
        flops=1 << 26,
    )
    return (q_core.reshape(HALF, 32, R + RZ), r_factor)


def solution(mesh):
    in_specs = (
        P(("sys", "rank"), "mode", None),
        P("sys", "rank", "mode", None),
        P("sys", None, "rank"),
        P("sys", None, None),
        P(("sys", "rank"), None),
        P("sys", "mode", None),
        P("sys", None),
    )
    out_specs = (P(("sys", "rank"), "mode", None), P("sys", None))
    return jax.shard_map(per_device, mesh=mesh, in_specs=in_specs, out_specs=out_specs, check_vma=False)
```

time: 80.3 us -> 55.2 us (0.69)
  Pallas kernels: 0 us -> 19.9 us
  blocking collectives: 29.7 us -> 11.3 us
  other arithmetic: 17.9 us -> 1.91 us
  local copies, waits for them, and re-layouts: 13.8 us -> 2.43 us
  starting transfers between devices: 3.49 us -> 8.62 us
  matrix products: 5.98 us -> 3.7 us
  waiting for transfers between devices: 8.11 us -> 6.28 us
    all_to_all x2 -> x0, blocking collectives: 21 us -> none  [the longest x1 16.8 us: from_everyone(): lax.all_to_all(jnp.broadcast_to(value[None], (length, *value.shape)), axi...]
    pallas_call x0 -> x5, Pallas kernels: none -> 19.9 us  [call(): pl.pallas_call(body, out_shape=outs, scratch_shapes=scratch, interpret=IN...]
    another operation x4 -> x0, other arithmetic: 14.1 us -> none  [the longest x3 7.98 us: per_device(): lower = jnp.linalg.cholesky(gram)]
    all_to_all x1 -> x2, starting transfers between devices: 3.49 us -> 8.62 us  [the longest x1 5.15 us: per_device(): lax.all_to_all(send, ('mode', 'rank'), split_axis=0, concat_axis=0, tiled...]
    unnamed x16 -> x14, local copies, waits for them, and re-layouts: 6.45 us -> 1.45 us
    all_to_all x1 -> x0, other arithmetic: 2.82 us -> none  [sum_at_owner(): lax.all_to_all(parts, axis, split_axis=0, concat_axis=0, tiled=True)]
    all_gather x1 -> x2, blocking collectives: 8.69 us -> 11.3 us  [the longest x1 8.87 us: per_device(): both = lax.all_gather(jnp.concatenate([sol, left], axis=0), 'rank', axis=0)]
    convert_element_type x1 -> x0, local copies, waits for them, and re-layouts: 2.21 us -> none  [per_device(): projected = jnp.einsum('cjd,dyb->cjyb', solution_core, right_interface, p...]
  transfers between devices with their start and end apart: 1 -> 2, of which waited for: 1 -> 1; matrix products, arithmetic and copies ran while one was open for 0% -> 3% of each run, Pallas kernels for 0% -> 14%
where the time goes in v1:
time: 55.2 us; the launch traced here: 54.8 us
  Pallas kernels  19.9 us (36%)
  blocking collectives  11.3 us (20%)
  starting transfers between devices  8.62 us (16%)
  waiting for transfers between devices  6.28 us (11%)
  matrix products  3.7 us (7%)
  local copies, waits for them, and re-layouts  2.43 us (4%)
  other arithmetic  1.91 us (3%)
  between operations  0.75 us (1%)
    pallas_call x5, Pallas kernels, call(): pl.pallas_call(body, out_shape=outs, scratch_shapes=scratch, interpret=IN...  19.9 us
    all_gather x1, blocking collectives, per_device(): both = lax.all_gather(jnp.concatenate([sol, left], axis=0), 'rank', axis=0)  8.87 us
    all_to_all x1, waiting for transfers between devices, per_device(): recv = lax.all_to_all(send, 'mode', split_axis=0, concat_axis=0, tiled=True)  6.28 us
    all_to_all x1, starting transfers between devices, per_device(): lax.all_to_all(send, ('mode', 'rank'), split_axis=0, concat_axis=0, tiled...  5.15 us
    all_to_all x1, starting transfers between devices, per_device(): recv = lax.all_to_all(send, 'mode', split_axis=0, concat_axis=0, tiled=True)  3.47 us
    dot_general x1, matrix products, per_device(): jnp.einsum('cxa,cxib->aib', left, applied, preferred_element_type=F32)  3.1 us
    all_gather x1, blocking collectives, per_device(): everyone = lax.all_gather(packed, 'rank', axis=0)  2.38 us
    unnamed x14, local copies, waits for them, and re-layouts  1.45 us
  transfers between devices with their start and end apart: 2, of which 1 were waited for; matrix products, arithmetic and copies ran while one was open for 3% of the time, Pallas kernels for 14%

profile of v1, /device:TPU:1, one launch (start us, length us, event | category | flops | bytes accessed | tf_op | source)
XLA Modules:
  0.0 54.8 jit_solution(15165571653323274220)
XLA Ops:
  0.6 0.0 copy-start
  0.6 1.1 %pad_maximum_fusion.1 = bf16[1280,64]{1,0:T(8,128)(2,1)S(1)} fusion(bf16[256,64]{1,0:T(8,128)(2,1)} %bitcast.78, bf16[1024,64]{1,0:T(8,128)(2,1)} %bitcast.72), kind=kLoop, calls=%fused_computation.9 | loop fusion | flops 327680 | bytes 327680 | tf_op jit(solution)/shard_map/concatenate | solution.py:136
  1.8 8.9 %all-gather = bf16[2560,64]{1,0:T(8,128)(2,1)} all-gather(bf16[1280,64]{1,0:T(8,128)(2,1)S(1)} %pad_maximum_fusion.1), channel_id=2, replica_groups=mesh['sys'=32,'mode'=8,'rank'=2] {'rank'}, dimensions={0}, use_global_device_ids=true | all-gather | bytes 491520 | tf_op jit(solution)/shard_map/all_gather | solution.py:136
  10.6 3.2 %shard_map.86 = (bf16[32,128,64]{2,1,0:T(8,128)(2,1)}, bf16[8,64,64]{2,1,0:T(8,128)(2,1)}, bf16[96,128]{1,0:T(8,128)(2,1)}) custom-call(bf16[2,1280,64]{2,1,0:T(8,128)(2,1)} %bitcast.69, bf16[128,64]{1,0:T(8,128)(2,1)} %bitcast.79), custom_call_target="tpu_custom_call" | custom-call | flops 67108864 | bytes 1048576 | tf_op jit(solution)/shard_map/pallas_call | solution.py:23
  13.8 3.1 %fusion.8.part_ref = bf16[16,64,128]{2,1,0:T(8,128)(2,1)} fusion(bf16[64,32,8,16,1]{0,3,2,1,4:T(8,128)(2,1)} %bitcast.77, bf16[8,128,32,8]{1,3,2,0:T(8,128)(2,1)S(1)} %copy-done, bf16[8,64,64]{2,1,0:T(8,128)(2,1)} %get-tuple-element.12), kind=kOutput, calls=%fused_computation.5 | convolution fusion | flops 672268288 | bytes 1376256 | tf_op jit(solution)/shard_map/cxa,cxib->aib/dot_general | solution.py:149
  16.9 1.9 %shard_map.87 = bf16[2,4,128,128]{3,2,1,0:T(8,128)(2,1)} custom-call(bf16[16,64,128]{2,1,0:T(8,128)(2,1)} %fusion.8.part_ref), custom_call_target="tpu_custom_call" | custom-call | flops 16777216 | bytes 1048576 | tf_op jit(solution)/shard_map/pallas_call | solution.py:23
  18.8 2.4 %all-gather.1 = bf16[4,4,128,128]{3,2,1,0:T(8,128)(2,1)S(1)} all-gather(bf16[2,4,128,128]{3,2,1,0:T(8,128)(2,1)} %shard_map.87), channel_id=3, replica_groups=mesh['sys'=32,'mode'=8,'rank'=2] {'rank'}, dimensions={0}, use_global_device_ids=true | all-gather | bytes 786432 | tf_op jit(solution)/shard_map/all_gather | solution.py:152
  21.2 0.0 copy-start.3
  21.3 0.0 copy-start.6
  21.3 0.0 copy-start.5
  21.3 0.8 %pad_maximum_fusion = bf16[8,224,128]{2,1,0:T(8,128)(2,1)} fusion(bf16[8,96,128]{2,1,0:T(8,128)(2,1)S(1)} %broadcast_in_dim.2, bf16[8,128,128]{2,1,0:T(8,128)(2,1)S(1)} %bitcast.71), kind=kLoop, calls=%fused_computation.8 | loop fusion | flops 917504 | bytes 917504 | tf_op jit(solution)/shard_map/concatenate | solution.py:154
  22.1 3.5 %all-to-all-start = ((bf16[8,224,128]{2,1,0:T(8,128)(2,1)}), bf16[8,224,128]{2,1,0:T(8,128)(2,1)S(1)}, u32[]{:S(2)}, u32[]{:S(2)}) async-start(bf16[8,224,128]{2,1,0:T(8,128)(2,1)} %pad_maximum_fusion), calls=%async_computation | async-start | bytes 917504 | tf_op jit(solution)/shard_map/all_to_all | solution.py:157
  25.6 0.2 fusion.19
  25.8 0.4 fusion.16
  26.3 0.1 copy.14
  26.4 0.8 %reshape.36.rhs_ref = f32[128,128]{1,0:T(8,128)} reshape(f32[4,32,4,32]{3,2,1,0:T(4,128)S(1)} %bitcast.75) | data formatting | bytes 131072 | tf_op jit(solution)/shard_map/reshape | solution.py:161
  27.2 6.3 %all-to-all-done.recv_ref = bf16[8,224,128]{2,1,0:T(8,128)(2,1)S(1)} async-done(((bf16[8,224,128]{2,1,0:T(8,128)(2,1)}), bf16[8,224,128]{2,1,0:T(8,128)(2,1)S(1)}, u32[]{:S(2)}, u32[]{:S(2)}) %all-to-all-start) | async-done | bytes 458784 | tf_op jit(solution)/shard_map/all_to_all | solution.py:157
  33.5 0.8 %copy-done.1 = bf16[8,224,128]{2,1,0:T(8,128)(2,1)} copy-done((bf16[8,224,128]{2,1,0:T(8,128)(2,1)}, bf16[8,224,128]{2,1,0:T(8,128)(2,1)S(1)}, u32[]{:S(2)}) %copy-start.1) | copy-done | bytes 458776
  34.2 2.4 %shard_map.88 = (f32[16,1024]{1,0:T(8,128)}, f32[16,16,128]{2,1,0:T(8,128)}, f32[64,64]{1,0:T(8,128)}) custom-call(bf16[8,224,128]{2,1,0:T(8,128)(2,1)} %copy-done.1, f32[128,128]{1,0:T(8,128)} %reshape.36.rhs_ref, bf16[1024,64]{1,0:T(8,128)(2,1)} %bitcast.73), custom_call_target="tpu_custom_call" | custom-call | flops 16777216 | bytes 1048576 | tf_op jit(solution)/shard_map/pallas_call | solution.py:23
  36.6 5.1 %all-to-all-start.1 = ((f32[16,16,128]{2,1,0:T(8,128)}), f32[16,16,128]{2,1,0:T(8,128)S(1)}, u32[]{:S(2)}, u32[]{:S(2)}) async-start(f32[16,16,128]{2,1,0:T(8,128)} %get-tuple-element.15), calls=%async_computation.1 | async-start | bytes 262144 | tf_op jit(solution)/shard_map/all_to_all | solution.py:171
  41.8 7.8 %shard_map.89 = (f32[64,128]{1,0:T(8,128)}, f32[1024,80]{1,0:T(8,128)}) custom-call(f32[64,64]{1,0:T(8,128)} %get-tuple-element.16.gram_ref, bf16[1024,64]{1,0:T(8,128)(2,1)} %bitcast.74, f32[16,1024]{1,0:T(8,128)} %get-tuple-element.17.turned_ref), custom_call_target="tpu_custom_call" | custom-call | flops 4294967296 | bytes 1048576 | tf_op jit(solution)/shard_map/pallas_call | solution.py:23
  49.6 0.0 all-to-all-done.1.recv_ref
  49.6 0.6 %copy-done.2 = f32[16,16,128]{2,1,0:T(8,128)} copy-done((f32[16,16,128]{2,1,0:T(8,128)}, f32[16,16,128]{2,1,0:T(8,128)S(1)}, u32[]{:S(2)}) %copy-start.2) | copy-done | bytes 131096
  50.2 4.6 %shard_map.90 = (f32[1024,80]{1,0:T(8,128)}, f32[80,80]{1,0:T(8,128)}) custom-call(f32[16,16,128]{2,1,0:T(8,128)} %copy-done.2, f32[64,128]{1,0:T(8,128)} %get-tuple-element.18.both_ref, f32[1024,80]{1,0:T(8,128)} %get-tuple-element.19.rows_ref), custom_call_target="tpu_custom_call" | custom-call | flops 67108864 | bytes 1048576 | tf_op jit(solution)/shard_map/pallas_call | solution.py:23
  (10 shorter events, 0.1 us)
Async XLA Ops:
  0.6 13.2 %copy-start = (bf16[8,128,32,8]{1,3,2,0:T(8,128)(2,1)S(1)}, bf16[8,128,32,8]{1,3,2,0:T(8,128)(2,1)}, u32[]{:S(2)}) copy-start(bf16[8,128,32,8]{1,3,2,0:T(8,128)(2,1)} %param.8) | copy-start | bytes 1572868
  16.9 4.4 %copy-start.4 = (bf16[96,128]{1,0:T(8,128)(2,1)S(1)}, bf16[96,128]{1,0:T(8,128)(2,1)}, u32[]{:S(2)}) copy-start(bf16[96,128]{1,0:T(8,128)(2,1)} %get-tuple-element.14) | copy-start | bytes 73732
  21.2 4.4 %copy-start.3 = (bf16[16,32,16]{1,2,0:T(8,128)(2,1)S(1)}, bf16[16,32,16]{1,2,0:T(8,128)(2,1)}, u32[]{:S(2)}) copy-start(bf16[16,32,16]{1,2,0:T(8,128)(2,1)} %param.12) | copy-start | bytes 49156
  21.3 4.4 %copy-start.6 = (bf16[16,16]{1,0:T(8,128)(2,1)S(1)}, bf16[16,16]{1,0:T(8,128)(2,1)}, u32[]{:S(2)}) copy-start(bf16[16,16]{1,0:T(8,128)(2,1)} %param.13) | copy-start | bytes 1540
  21.3 4.5 %copy-start.5 = (bf16[32,16]{0,1:T(8,128)(2,1)S(1)}, bf16[32,16]{0,1:T(8,128)(2,1)}, u32[]{:S(2)}) copy-start(bf16[32,16]{0,1:T(8,128)(2,1)} %param.11) | copy-start | bytes 3076
  22.1 11.3 %all-to-all-start = ((bf16[8,224,128]{2,1,0:T(8,128)(2,1)}), bf16[8,224,128]{2,1,0:T(8,128)(2,1)S(1)}, u32[]{:S(2)}, u32[]{:S(2)}) async-start(bf16[8,224,128]{2,1,0:T(8,128)(2,1)} %pad_maximum_fusion), calls=%async_computation | async-start | bytes 917504 | tf_op jit(solution)/shard_map/all_to_all | solution.py:157
  33.5 0.8 %copy-start.1 = (bf16[8,224,128]{2,1,0:T(8,128)(2,1)}, bf16[8,224,128]{2,1,0:T(8,128)(2,1)S(1)}, u32[]{:S(2)}) copy-start(bf16[8,224,128]{2,1,0:T(8,128)(2,1)S(1)} %all-to-all-done.recv_ref) | copy-start | bytes 1376260
  36.6 13.0 %all-to-all-start.1 = ((f32[16,16,128]{2,1,0:T(8,128)}), f32[16,16,128]{2,1,0:T(8,128)S(1)}, u32[]{:S(2)}, u32[]{:S(2)}) async-start(f32[16,16,128]{2,1,0:T(8,128)} %get-tuple-element.15), calls=%async_computation.1 | async-start | bytes 262144 | tf_op jit(solution)/shard_map/all_to_all | solution.py:171
  49.6 0.7 %copy-start.2 = (f32[16,16,128]{2,1,0:T(8,128)}, f32[16,16,128]{2,1,0:T(8,128)S(1)}, u32[]{:S(2)}) copy-start(f32[16,16,128]{2,1,0:T(8,128)S(1)} %all-to-all-done.1.recv_ref) | copy-start | bytes 393220

commit v2 on v1

--- a/solution.py
+++ b/solution.py
@@ -25,6 +25,9 @@
         out_shape=outs,
         scratch_shapes=scratch,
         interpret=INTERPRET,
+        compiler_params=pltpu.CompilerParams(vmem_limit_bytes=12 << 20),
+        in_specs=[pl.BlockSpec(memory_space=pltpu.VMEM)] * len(args),
+        out_specs=jax.tree.map(lambda _: pl.BlockSpec(memory_space=pltpu.VMEM), outs),
         cost_estimate=pl.CostEstimate(flops=flops, bytes_accessed=1 << 20, transcendentals=0),
         **kw,
     )(*args)

time: 55.2 us -> 44 us (0.80)
  Pallas kernels: 19.9 us -> 12.2 us
  local copies, waits for them, and re-layouts: 2.43 us -> 0.39 us
  matrix products: 3.7 us -> 1.7 us
  waiting for transfers between devices: 6.28 us -> 7.01 us
    pallas_call x5, Pallas kernels: 19.9 us -> 12.2 us  [call(): pl.pallas_call(body, out_shape=outs, scratch_shapes=scratch, interpret=IN...]
    dot_general x1, matrix products: 3.1 us -> 1.1 us  [per_device(): jnp.einsum('cxa,cxib->aib', left, applied, preferred_element_type=F32)]
    unnamed x14 -> x12, local copies, waits for them, and re-layouts: 1.45 us -> 0.04 us
    reshape x1, local copies, waits for them, and re-layouts: 0.78 us -> 0.16 us  [per_device(): jnp.transpose(rhs_term.reshape(HALF, 32, 4, 4), (2, 0, 3, 1))]
    all_to_all x1, waiting for transfers between devices: 6.28 us -> 6.89 us  [per_device(): recv = lax.all_to_all(send, 'mode', split_axis=0, concat_axis=0, tiled=True)]
  transfers between devices with their start and end apart: 2 -> 2, of which waited for: 1 -> 2; matrix products, arithmetic and copies ran while one was open for 3% -> 2% of each run, Pallas kernels for 14% -> 14%
where the time goes in v2:
time: 44 us; the launch traced here: 43.7 us
  Pallas kernels  12.2 us (28%)
  blocking collectives  10.9 us (25%)
  starting transfers between devices  8.75 us (20%)
  waiting for transfers between devices  7.01 us (16%)
  other arithmetic  1.91 us (4%)
  matrix products  1.7 us (4%)
  between operations  0.79 us (2%)
    pallas_call x5, Pallas kernels, call(): pl.pallas_call(body, out_shape=outs, scratch_shapes=scratch, interpret=IN...  12.2 us
    all_gather x1, blocking collectives, per_device(): both = lax.all_gather(jnp.concatenate([sol, left], axis=0), 'rank', axis=0)  8.74 us
    all_to_all x1, waiting for transfers between devices, per_device(): recv = lax.all_to_all(send, 'mode', split_axis=0, concat_axis=0, tiled=True)  6.89 us
    all_to_all x1, starting transfers between devices, per_device(): lax.all_to_all(send, ('mode', 'rank'), split_axis=0, concat_axis=0, tiled...  5.14 us
    all_to_all x1, starting transfers between devices, per_device(): recv = lax.all_to_all(send, 'mode', split_axis=0, concat_axis=0, tiled=True)  3.61 us
    all_gather x1, blocking collectives, per_device(): everyone = lax.all_gather(packed, 'rank', axis=0)  2.18 us
    concatenate x1, other arithmetic, per_device(): both = lax.all_gather(jnp.concatenate([sol, left], axis=0), 'rank', axis=0)  1.11 us
    dot_general x1, matrix products, per_device(): jnp.einsum('cxa,cxib->aib', left, applied, preferred_element_type=F32)  1.1 us
  transfers between devices with their start and end apart: 2, of which 2 were waited for; matrix products, arithmetic and copies ran while one was open for 2% of the time, Pallas kernels for 14%

profile of v2, /device:TPU:1, one launch (start us, length us, event | category | flops | bytes accessed | tf_op | source)
XLA Modules:
  0.0 43.7 jit_solution(16180579680929551091)
XLA Ops:
  0.6 0.0 copy-start
  0.7 1.1 %pad_maximum_fusion.1 = bf16[1280,64]{1,0:T(8,128)(2,1)S(1)} fusion(bf16[256,64]{1,0:T(8,128)(2,1)} %bitcast.79, bf16[1024,64]{1,0:T(8,128)(2,1)} %bitcast.70), kind=kLoop, calls=%fused_computation.9 | loop fusion | flops 327680 | bytes 327680 | tf_op jit(solution)/shard_map/concatenate | solution.py:139
  1.8 8.7 %all-gather = bf16[2560,64]{1,0:T(8,128)(2,1)S(1)} all-gather(bf16[1280,64]{1,0:T(8,128)(2,1)S(1)} %pad_maximum_fusion.1), channel_id=2, replica_groups=mesh['sys'=32,'mode'=8,'rank'=2] {'rank'}, dimensions={0}, use_global_device_ids=true | all-gather | bytes 491520 | tf_op jit(solution)/shard_map/all_gather | solution.py:139
  10.5 1.2 %shard_map.86 = (bf16[32,128,64]{2,1,0:T(8,128)(2,1)S(1)}, bf16[8,64,64]{2,1,0:T(8,128)(2,1)S(1)}, bf16[96,128]{1,0:T(8,128)(2,1)S(1)}) custom-call(bf16[2,1280,64]{2,1,0:T(8,128)(2,1)S(1)} %bitcast.69, bf16[128,64]{1,0:T(8,128)(2,1)S(1)} %bitcast.74), custom_call_target="tpu_custom_call" | custom-call | flops 67108864 | bytes 1048576 | tf_op jit(solution)/shard_map/pallas_call | solution.py:23
  11.7 0.0 copy-done
  11.7 1.1 %fusion.8.part_ref = bf16[16,64,128]{2,1,0:T(8,128)(2,1)S(1)} fusion(bf16[64,32,8,16,1]{0,3,2,1,4:T(8,128)(2,1)S(1)} %bitcast.73, bf16[8,128,32,8]{1,3,2,0:T(8,128)(2,1)S(1)} %copy-done, bf16[8,64,64]{2,1,0:T(8,128)(2,1)S(1)} %get-tuple-element.12), kind=kOutput, calls=%fused_computation.5 | convolution fusion | flops 672268288 | bytes 1376256 | tf_op jit(solution)/shard_map/cxa,cxib->aib/dot_general | solution.py:152
  12.8 0.3 shard_map.87
  13.1 2.2 %all-gather.1 = bf16[4,4,128,128]{3,2,1,0:T(8,128)(2,1)S(1)} all-gather(bf16[2,4,128,128]{3,2,1,0:T(8,128)(2,1)S(1)} %shard_map.87), channel_id=3, replica_groups=mesh['sys'=32,'mode'=8,'rank'=2] {'rank'}, dimensions={0}, use_global_device_ids=true | all-gather | bytes 786432 | tf_op jit(solution)/shard_map/all_gather | solution.py:155
  15.3 0.0 copy-start.3
  15.3 0.0 copy-start.5
  15.4 0.0 copy-start.4
  15.4 0.8 %pad_maximum_fusion = bf16[8,224,128]{2,1,0:T(8,128)(2,1)} fusion(bf16[8,96,128]{2,1,0:T(8,128)(2,1)S(1)} %broadcast_in_dim.2, bf16[8,128,128]{2,1,0:T(8,128)(2,1)S(1)} %bitcast.76), kind=kLoop, calls=%fused_computation.8 | loop fusion | flops 917504 | bytes 917504 | tf_op jit(solution)/shard_map/concatenate | solution.py:157
  16.2 3.6 %all-to-all-start = ((bf16[8,224,128]{2,1,0:T(8,128)(2,1)}), bf16[8,224,128]{2,1,0:T(8,128)(2,1)S(1)}, u32[]{:S(2)}, u32[]{:S(2)}) async-start(bf16[8,224,128]{2,1,0:T(8,128)(2,1)} %pad_maximum_fusion), calls=%async_computation | async-start | bytes 917504 | tf_op jit(solution)/shard_map/all_to_all | solution.py:160
  19.8 0.2 fusion.19
  20.0 0.0 copy-done.4
  20.0 0.4 fusion.16
  20.4 0.1 copy.14
  20.6 0.2 reshape.36.rhs_ref
  20.8 6.9 %all-to-all-done.recv_ref = bf16[8,224,128]{2,1,0:T(8,128)(2,1)S(1)} async-done(((bf16[8,224,128]{2,1,0:T(8,128)(2,1)}), bf16[8,224,128]{2,1,0:T(8,128)(2,1)S(1)}, u32[]{:S(2)}, u32[]{:S(2)}) %all-to-all-start) | async-done | bytes 458784 | tf_op jit(solution)/shard_map/all_to_all | solution.py:160
  27.7 1.2 %shard_map.88 = (f32[16,1024]{1,0:T(8,128)S(1)}, f32[16,16,128]{2,1,0:T(8,128)}, f32[64,64]{1,0:T(8,128)S(1)}) custom-call(bf16[8,224,128]{2,1,0:T(8,128)(2,1)S(1)} %all-to-all-done.recv_ref, f32[128,128]{1,0:T(8,128)S(1)} %reshape.36.rhs_ref, bf16[1024,64]{1,0:T(8,128)(2,1)S(1)} %bitcast.71), custom_call_target="tpu_custom_call" | custom-call | flops 16777216 | bytes 1048576 | tf_op jit(solution)/shard_map/pallas_call | solution.py:23
  28.9 5.1 %all-to-all-start.1 = ((f32[16,16,128]{2,1,0:T(8,128)}), f32[16,16,128]{2,1,0:T(8,128)S(1)}, u32[]{:S(2)}, u32[]{:S(2)}) async-start(f32[16,16,128]{2,1,0:T(8,128)} %get-tuple-element.15), calls=%async_computation.1 | async-start | bytes 262144 | tf_op jit(solution)/shard_map/all_to_all | solution.py:174
  34.1 6.1 %shard_map.89 = (f32[64,128]{1,0:T(8,128)S(1)}, f32[1024,80]{1,0:T(8,128)S(1)}) custom-call(f32[64,64]{1,0:T(8,128)S(1)} %get-tuple-element.16.gram_ref, bf16[1024,64]{1,0:T(8,128)(2,1)S(1)} %bitcast.72, f32[16,1024]{1,0:T(8,128)S(1)} %get-tuple-element.17.turned_ref), custom_call_target="tpu_custom_call" | custom-call | flops 4294967296 | bytes 1048576 | tf_op jit(solution)/shard_map/pallas_call | solution.py:23
  40.1 0.1 all-to-all-done.1.recv_ref
  40.3 3.4 %shard_map.90 = (f32[1024,80]{1,0:T(8,128)}, f32[80,80]{1,0:T(8,128)}) custom-call(f32[16,16,128]{2,1,0:T(8,128)S(1)} %all-to-all-done.1.recv_ref, f32[64,128]{1,0:T(8,128)S(1)} %get-tuple-element.18.both_ref, f32[1024,80]{1,0:T(8,128)S(1)} %get-tuple-element.19.rows_ref), custom_call_target="tpu_custom_call" | custom-call | flops 67108864 | bytes 1048576 | tf_op jit(solution)/shard_map/pallas_call | solution.py:23
  (8 shorter events, 0.1 us)
Async XLA Ops:
  0.6 11.1 %copy-start = (bf16[8,128,32,8]{1,3,2,0:T(8,128)(2,1)S(1)}, bf16[8,128,32,8]{1,3,2,0:T(8,128)(2,1)}, u32[]{:S(2)}) copy-start(bf16[8,128,32,8]{1,3,2,0:T(8,128)(2,1)} %param.8) | copy-start | bytes 1572868
  0.6 9.9 %copy-start.2 = (bf16[64,8,16]{0,2,1:T(8,128)(2,1)S(1)}, bf16[64,8,16]{0,2,1:T(8,128)(2,1)}, u32[]{:S(2)}) copy-start(bf16[64,8,16]{0,2,1:T(8,128)(2,1)} %param.10) | copy-start | bytes 49156
  15.3 4.5 %copy-start.3 = (bf16[16,32,16]{1,2,0:T(8,128)(2,1)S(1)}, bf16[16,32,16]{1,2,0:T(8,128)(2,1)}, u32[]{:S(2)}) copy-start(bf16[16,32,16]{1,2,0:T(8,128)(2,1)} %param.12) | copy-start | bytes 49156
  15.3 4.5 %copy-start.5 = (bf16[16,16]{1,0:T(8,128)(2,1)S(1)}, bf16[16,16]{1,0:T(8,128)(2,1)}, u32[]{:S(2)}) copy-start(bf16[16,16]{1,0:T(8,128)(2,1)} %param.13) | copy-start | bytes 1540
  15.4 4.6 %copy-start.4 = (bf16[32,16]{0,1:T(8,128)(2,1)S(1)}, bf16[32,16]{0,1:T(8,128)(2,1)}, u32[]{:S(2)}) copy-start(bf16[32,16]{0,1:T(8,128)(2,1)} %param.11) | copy-start | bytes 3076
  16.2 11.5 %copy-start.1 = (bf16[32,32,64]{2,1,0:T(8,128)(2,1)S(1)}, bf16[32,32,64]{2,1,0:T(8,128)(2,1)}, u32[]{:S(2)}) copy-start(bf16[32,32,64]{2,1,0:T(8,128)(2,1)} %param.7) | copy-start | bytes 393220
  16.2 11.5 %all-to-all-start = ((bf16[8,224,128]{2,1,0:T(8,128)(2,1)}), bf16[8,224,128]{2,1,0:T(8,128)(2,1)S(1)}, u32[]{:S(2)}, u32[]{:S(2)}) async-start(bf16[8,224,128]{2,1,0:T(8,128)(2,1)} %pad_maximum_fusion), calls=%async_computation | async-start | bytes 917504 | tf_op jit(solution)/shard_map/all_to_all | solution.py:160
  28.9 11.3 %all-to-all-start.1 = ((f32[16,16,128]{2,1,0:T(8,128)}), f32[16,16,128]{2,1,0:T(8,128)S(1)}, u32[]{:S(2)}, u32[]{:S(2)}) async-start(f32[16,16,128]{2,1,0:T(8,128)} %get-tuple-element.15), calls=%async_computation.1 | async-start | bytes 262144 | tf_op jit(solution)/shard_map/all_to_all | solution.py:174

commit v3 on v1

v3 whole, which is shorter than its diff:
```python
import jax
import jax.numpy as jnp
from jax import lax
from jax.experimental import pallas as pl
from jax.experimental.pallas import tpu as pltpu
from jax.sharding import PartitionSpec as P

INTERPRET = False
F32 = jnp.float32
BF16 = jnp.bfloat16
HIGHEST = lax.Precision.HIGHEST

R = 64
RZ = 16
RA = 8
HALF = 32
ROWS = 1024
NT = (((1,), (1,)), ((), ()))
TN = (((0,), (0,)), ((), ()))


VMEM = pl.BlockSpec(memory_space=pltpu.VMEM)


def call(body, outs, *args, scratch=(), flops=0, in_specs=None):
    return pl.pallas_call(
        body,
        out_shape=outs,
        in_specs=in_specs or [VMEM] * len(args),
        out_specs=jax.tree.map(lambda _: VMEM, outs),
        scratch_shapes=scratch,
        interpret=INTERPRET,
        compiler_params=pltpu.CompilerParams(vmem_limit_bytes=12 << 20),
        cost_estimate=pl.CostEstimate(flops=flops, bytes_accessed=1 << 20, transcendentals=0),
    )(*args)


def in_hbm(x):
    return x if INTERPRET else pltpu.with_memory_space_constraint(x, pltpu.HBM)


def three_parts(x):
    hi = x.astype(BF16)
    rest = x - hi.astype(F32)
    mid = rest.astype(BF16)
    return hi, mid, (rest - mid.astype(F32)).astype(BF16)


def join(sol_ref, left_ref, out_ref, sem):
    copies = [
        pltpu.make_async_copy(sol_ref, out_ref.at[0:ROWS], sem.at[0]),
        pltpu.make_async_copy(left_ref, out_ref.at[ROWS : ROWS + RA * HALF], sem.at[1]),
    ]
    for copy in copies:
        copy.start()
    for copy in copies:
        copy.wait()


def same(rows, lanes, row_of, lane_of):
    row = lax.broadcasted_iota(jnp.int32, (rows, lanes), 0)
    lane = lax.broadcasted_iota(jnp.int32, (rows, lanes), 1)
    return row_of(row) == lane_of(lane)


def project(both_ref, right_ref, rhs_left_ref, rhs_core_ref, rhs_right_ref, proj_ref, left_ref, gram_ref, rhs_ref, sol_ref):
    sol_ref[0:ROWS] = both_ref[0, 0:ROWS].astype(F32)
    sol_ref[ROWS : 2 * ROWS] = both_ref[1, 0:ROWS].astype(F32)
    right = right_ref[...]
    for j in range(32):
        rows = sol_ref[pl.ds(j, R, stride=32), :].astype(BF16)
        proj_ref[j] = lax.dot_general(right, rows, NT, preferred_element_type=F32).astype(BF16)
    for x in range(RA):
        for r in range(2):
            left_ref[x, HALF * r : HALF * (r + 1)] = both_ref[r, ROWS + HALF * x : ROWS + HALF * (x + 1)]
    gram = jnp.zeros((R, R), F32)
    for r in range(2):
        s = both_ref[r, 0:ROWS]
        gram = gram + lax.dot_general(s, s, TN, preferred_element_type=F32)
    for p, part in enumerate(three_parts(gram)):
        part = part.astype(F32)
        gram_ref[HALF * p : HALF * (p + 1)] = jnp.concatenate([part[:HALF], part[HALF:]], axis=1).astype(BF16)
    group = lax.broadcasted_iota(jnp.int32, (HALF, 128), 1) >> 4
    turned = jnp.concatenate([rhs_right_ref[...].astype(F32).T] * 8, axis=1)
    turned = jnp.broadcast_to(turned[:, None, :], (16, 16, 128)).reshape(256, 128)
    row = lax.broadcasted_iota(jnp.int32, (256, 128), 0) & 15
    lane = lax.broadcasted_iota(jnp.int32, (256, 128), 1) >> 4
    spread = jnp.concatenate([jnp.where(row == lane + 8 * h, turned, 0.0) for h in range(2)], axis=1).astype(BF16)
    half_done = jnp.dot(spread, rhs_core_ref[...], preferred_element_type=F32)
    turned = jnp.concatenate([rhs_left_ref[...].astype(F32).T] * 8, axis=1)
    blank = jnp.zeros((HALF, 128), F32)
    spread = []
    for b in range(RZ):
        tile = jnp.where(group == b % 8, turned, 0.0)
        spread.append(jnp.concatenate([tile, blank] if b < 8 else [blank, tile], axis=1))
    spread = jnp.concatenate(spread, axis=0).astype(BF16)
    total = jnp.zeros((512, 32), F32)
    for part in three_parts(half_done):
        total = total + jnp.dot(spread, part, preferred_element_type=F32)
    rhs_ref[...] = total


def pack(rank_ref, part_ref, keep_ref, give_ref):
    rank = rank_ref[0]
    for out_ref, half in ((keep_ref, rank), (give_ref, 1 - rank)):
        rows = pl.ds(pl.multiple_of(HALF * half, HALF), HALF)
        for g in range(4):
            four = [part_ref[4 * g + k, rows, :].astype(F32) for k in range(4)]
            for q in range(4):
                piece = jnp.concatenate([x[:, 32 * q : 32 * (q + 1)] for x in four], axis=1)
                out_ref[q, HALF * g : HALF * (g + 1)] = piece.astype(BF16)


def choose(rank_ref, keep_ref, every_ref, gram_ref, out_ref):
    rank = rank_ref[0]
    gram = gram_ref[...]
    for q in range(4):
        out_ref[4 * rank + q, 0:128] = keep_ref[q]
        out_ref[4 - 4 * rank + q, 0:128] = every_ref[1 - rank, q]
    for k in range(8):
        out_ref[k, 128:224] = gram


def residual(recv_ref, rhs_ref, sol_ref, turned_ref, send_ref, gram_ref, rows_ref):
    total = recv_ref[0].astype(F32)
    for m in range(1, 8):
        total = total + recv_ref[m].astype(F32)
    packed = total[128:160] + total[160:192] + total[192:224]
    gram_ref[0:HALF] = packed[:, 0:R]
    gram_ref[HALF:R] = packed[:, R:]
    for k in range(4):
        shifted = total[0:128] if k == 0 else pltpu.roll(total[0:128], 128 - 32 * k, 1)
        for g in range(4):
            rows = slice(HALF * (4 * g + k), HALF * (4 * g + k + 1))
            rows_ref[rows] = rhs_ref[rows] - shifted[HALF * g : HALF * (g + 1), :32]
    for t in range(8):
        four = [rows_ref[pl.ds(4 * t + s, RZ, stride=32), :] for s in range(4)]
        turned_ref[:, 128 * t : 128 * (t + 1)] = jnp.concatenate(four, axis=1)
    turned = turned_ref[...]
    stacked = jnp.concatenate(three_parts(turned), axis=0)
    cross = jnp.dot(stacked, sol_ref[...], preferred_element_type=F32)
    cross = cross[0:16] + cross[16:32] + cross[32:48]
    own = lax.dot_general(turned, turned, NT, precision=HIGHEST, preferred_element_type=F32)
    row = jnp.concatenate([cross, own, jnp.zeros((RZ, 48), F32)], axis=1)
    for k in range(16):
        send_ref[k] = row


def eliminate(m, n):
    index = lax.broadcasted_iota(jnp.int32, (n, 1), 0)
    for k in range(n):
        row = m[k : k + 1]
        factor = jnp.where(index > k, m[:, k : k + 1] / m[k : k + 1, k : k + 1], 0.0)
        m = m - factor * row
    lane = lax.broadcasted_iota(jnp.int32, m.shape, 1)
    pivot = jnp.sum(jnp.where(lane == index, m, 0.0), axis=1, keepdims=True)
    return m * lax.rsqrt(pivot)


def first_block(gram_ref, sol_ref, both_ref, ortho_ref, parts_ref):
    eye = same(R, R, lambda r: r, lambda l: l).astype(F32)
    both = eliminate(jnp.concatenate([gram_ref[...], eye], axis=1), R)
    both_ref[...] = both
    stacked = jnp.concatenate(three_parts(both[:, R:]), axis=0)
    ortho = lax.dot_general(stacked, sol_ref[...], NT, preferred_element_type=F32)
    ortho = ortho[0:R] + ortho[R : 2 * R] + ortho[2 * R :]
    ortho_ref[...] = ortho
    hi, mid, _ = three_parts(ortho)
    for k, part in enumerate((hi, mid, hi, mid)):
        parts_ref[R * k : R * (k + 1)] = part


def last_block(recv_ref, both_ref, ortho_ref, parts_ref, turned_ref, q_ref, r_ref):
    total = recv_ref[0]
    for k in range(1, 16):
        total = total + recv_ref[k]
    both = both_ref[...]
    cross = lax.dot_general(total[:, :R], both[:, R:], NT, precision=HIGHEST, preferred_element_type=F32)
    schur = total[:, R : R + RZ] - lax.dot_general(cross, cross, NT, precision=HIGHEST, preferred_element_type=F32)
    hi, mid, _ = three_parts(cross)
    wide = jnp.concatenate([hi, hi, mid, mid], axis=1)
    resid = turned_ref[...] - jnp.dot(wide, parts_ref[...], preferred_element_type=F32)
    blocks = [resid[:, 128 * t : 128 * (t + 1)] for t in range(8)]
    columns = [jnp.broadcast_to(schur[:, k : k + 1], (RZ, 128)) for k in range(RZ)]
    index = lax.broadcasted_iota(jnp.int32, (RZ, 128), 0)
    lane = lax.broadcasted_iota(jnp.int32, (RZ, 128), 1)
    pivots = jnp.zeros((RZ, 128), F32)
    upper = jnp.zeros((RZ, 128), F32)
    for k in range(RZ):
        pivots = jnp.where(index == k, columns[k], pivots)
        upper = jnp.where((lane == R + k) & (index <= k), columns[k], upper)
        factor = jnp.where(index > k, columns[k] / columns[k][k : k + 1], 0.0)
        for j in range(k + 1, RZ):
            columns[j] = columns[j] - factor * columns[j][k : k + 1]
        blocks = [x - factor * x[k : k + 1] for x in blocks]
    scale = lax.rsqrt(pivots)
    for t in range(8):
        lanes = slice(128 * t, 128 * (t + 1))
        q_ref[lanes] = jnp.concatenate([ortho_ref[:, lanes], blocks[t] * scale], axis=0).T
    r_ref[0:R] = jnp.concatenate([both[:, :R], cross.T], axis=1)
    r_ref[R:] = (upper * scale)[:, : R + RZ]


def per_device(solution_core, operator_core, left_interface, right_interface, rhs_left, rhs_core, rhs_right):
    shape = jax.ShapeDtypeStruct
    sol = solution_core.reshape(ROWS, R)
    left = jnp.transpose(left_interface, (1, 2, 0)).reshape(RA * HALF, R)
    hbm = pl.BlockSpec(memory_space=pltpu.HBM)
    own = call(
        join,
        shape((ROWS + RA * HALF, R), BF16),
        in_hbm(sol),
        in_hbm(left),
        scratch=[pltpu.SemaphoreType.DMA((2,))],
        in_specs=[hbm, hbm],
    )
    both = lax.all_gather(own, "rank", axis=0)
    right = jnp.transpose(right_interface, (1, 2, 0)).reshape(RA * RZ, R)
    proj, left, early, rhs_term = call(
        project,
        (
            shape((32, 128, R), BF16),
            shape((RA, R, R), BF16),
            shape((96, 128), BF16),
            shape((512, 32), F32),
        ),
        both,
        right,
        rhs_left.T,
        jnp.transpose(rhs_core, (0, 2, 1)).reshape(256, 32),
        rhs_right,
        scratch=[pltpu.VMEM((2 * ROWS, R), F32)],
        flops=1 << 26,
    )
    proj = jnp.transpose(proj.reshape(32, RA, RZ, R), (3, 0, 1, 2))
    left = jnp.transpose(left, (1, 0, 2))
    applied = jnp.einsum("xijy,cjyb->cxib", operator_core, proj, preferred_element_type=F32).astype(BF16)
    partial_value = jnp.einsum("cxa,cxib->aib", left, applied, preferred_element_type=F32)
    partial_value = jnp.transpose(partial_value, (2, 0, 1)).astype(BF16)
    rank = lax.axis_index("rank").astype(jnp.int32).reshape(1)
    smem = pl.BlockSpec(memory_space=pltpu.SMEM)
    chunks = shape((4, 128, 128), BF16)
    keep, give = call(pack, (chunks, chunks), rank, partial_value, flops=1 << 24, in_specs=[smem, VMEM])
    everyone = lax.all_gather(give, "rank", axis=0)
    send = call(
        choose,
        shape((8, 224, 128), BF16),
        rank,
        keep,
        everyone,
        early,
        in_specs=[smem, VMEM, VMEM, VMEM],
    )
    recv = lax.all_to_all(send, "mode", split_axis=0, concat_axis=0, tiled=True)
    turned, send, gram = call(
        residual,
        (shape((RZ, ROWS), F32), shape((16, RZ, 128), F32), shape((R, R), F32)),
        recv,
        rhs_term,
        sol,
        scratch=[pltpu.VMEM((512, 32), F32)],
        flops=1 << 24,
    )
    recv = lax.all_to_all(send, ("mode", "rank"), split_axis=0, concat_axis=0, tiled=True)
    factor, ortho, parts = call(
        first_block,
        (shape((R, 2 * R), F32), shape((R, ROWS), F32), shape((4 * R, ROWS), BF16)),
        gram,
        sol,
        flops=1 << 32,
    )
    q_core, r_factor = call(
        last_block,
        (shape((ROWS, R + RZ), F32), shape((R + RZ, R + RZ), F32)),
        recv,
        factor,
        ortho,
        parts,
        turned,
        flops=1 << 26,
    )
    return (q_core.reshape(HALF, 32, R + RZ), r_factor)


def solution(mesh):
    in_specs = (
        P(("sys", "rank"), "mode", None),
        P("sys", "rank", "mode", None),
        P("sys", None, "rank"),
        P("sys", None, None),
        P(("sys", "rank"), None),
        P("sys", "mode", None),
        P("sys", None),
    )
    out_specs = (P(("sys", "rank"), "mode", None), P("sys", None))
    return jax.shard_map(per_device, mesh=mesh, in_specs=in_specs, out_specs=out_specs, check_vma=False)
```

time: 55.2 us -> 41.2 us (0.75)
  blocking collectives: 11.3 us -> 21.6 us
  Pallas kernels: 19.9 us -> 11.6 us
  waiting for transfers between devices: 6.28 us -> 0.49 us
  starting transfers between devices: 8.62 us -> 5.34 us
  matrix products: 3.7 us -> 1.1 us
  local copies, waits for them, and re-layouts: 2.43 us -> 0.03 us
  other arithmetic: 1.91 us -> 0 us
    all_to_all x0 -> x1, blocking collectives: none -> 10.7 us  [per_device(): recv = lax.all_to_all(send, 'mode', split_axis=0, concat_axis=0, tiled=True)]
    pallas_call x5 -> x7, Pallas kernels: 19.9 us -> 11.6 us  [call(): pl.pallas_call(body, out_shape=outs, in_specs=in_specs or [VMEM] * len(ar...]
    all_to_all x1 -> x0, waiting for transfers between devices: 6.28 us -> none  [per_device(): recv = lax.all_to_all(send, 'mode', split_axis=0, concat_axis=0, tiled=True)]
    all_to_all x1 -> x0, starting transfers between devices: 3.47 us -> none  [per_device(): recv = lax.all_to_all(send, 'mode', split_axis=0, concat_axis=0, tiled=True)]
    dot_general x1, matrix products: 3.1 us -> 1.1 us  [per_device(): jnp.einsum('cxa,cxib->aib', left, applied, preferred_element_type=F32)]
    concatenate x2 -> x0, other arithmetic: 1.91 us -> none  [the longest x1 1.11 us: per_device(): both = lax.all_gather(jnp.concatenate([sol, left], axis=0), 'rank', axis=0)]
    unnamed x14 -> x12, local copies, waits for them, and re-layouts: 1.45 us -> 0.03 us
    reshape x2 -> x0, local copies, waits for them, and re-layouts: 0.93 us -> none  [the longest x1 0.78 us: per_device(): jnp.transpose(rhs_term.reshape(HALF, 32, 4, 4), (2, 0, 3, 1))]
  transfers between devices with their start and end apart: 2 -> 1, of which waited for: 1 -> 1; matrix products, arithmetic and copies ran while one was open for 3% -> 0% of each run, Pallas kernels for 14% -> 14%
where the time goes in v3:
time: 41.2 us; the launch traced here: 40.9 us
  blocking collectives  21.6 us (52%)
  Pallas kernels  11.6 us (28%)
  starting transfers between devices  5.34 us (13%)
  matrix products  1.1 us (3%)
  between operations  0.74 us (2%)
  waiting for transfers between devices  0.49 us (1%)
    pallas_call x7, Pallas kernels, call(): pl.pallas_call(body, out_shape=outs, in_specs=in_specs or [VMEM] * len(ar...  11.6 us
    all_to_all x1, blocking collectives, per_device(): recv = lax.all_to_all(send, 'mode', split_axis=0, concat_axis=0, tiled=True)  10.7 us
    all_gather x1, blocking collectives, per_device(): both = lax.all_gather(own, 'rank', axis=0)  8.74 us
    all_to_all x1, starting transfers between devices, per_device(): lax.all_to_all(send, ('mode', 'rank'), split_axis=0, concat_axis=0, tiled...  5.34 us
    all_gather x1, blocking collectives, per_device(): everyone = lax.all_gather(give, 'rank', axis=0)  2.14 us
    dot_general x1, matrix products, per_device(): jnp.einsum('cxa,cxib->aib', left, applied, preferred_element_type=F32)  1.1 us
  transfers between devices with their start and end apart: 1, of which 1 were waited for; matrix products, arithmetic and copies ran while one was open for 0% of the time, Pallas kernels for 14%

profile of v3, /device:TPU:1, one launch (start us, length us, event | category | flops | bytes accessed | tf_op | source)
XLA Modules:
  0.0 40.9 jit_solution(17828961553924384454)
XLA Ops:
  0.6 0.0 copy-start
  0.6 0.0 copy-start.3
  0.7 0.0 copy-start.4
  0.7 0.0 copy-start.2
  0.7 0.0 copy-start.5
  0.7 1.0 %shard_map.86 = bf16[1280,64]{1,0:T(8,128)(2,1)S(1)} custom-call(bf16[1024,64]{1,0:T(8,128)(2,1)} %bitcast.63, bf16[256,64]{1,0:T(8,128)(2,1)} %bitcast.69), custom_call_target="tpu_custom_call" | custom-call | bytes 1048576 | tf_op jit(solution)/shard_map/pallas_call | solution.py:26
  1.7 8.7 %all-gather = bf16[2560,64]{1,0:T(8,128)(2,1)S(1)} all-gather(bf16[1280,64]{1,0:T(8,128)(2,1)S(1)} %shard_map.86), channel_id=2, replica_groups=mesh['sys'=32,'mode'=8,'rank'=2] {'rank'}, dimensions={0}, use_global_device_ids=true | all-gather | bytes 491520 | tf_op jit(solution)/shard_map/all_gather | solution.py:217
  10.5 0.0 copy-done.3
  10.5 0.0 copy-done.4
  10.5 0.0 copy-done.2
  10.5 0.0 copy-done.5
  10.5 1.6 %shard_map.87 = (bf16[32,128,64]{2,1,0:T(8,128)(2,1)S(1)}, bf16[8,64,64]{2,1,0:T(8,128)(2,1)S(1)}, bf16[96,128]{1,0:T(8,128)(2,1)S(1)}, f32[512,32]{1,0:T(8,128)S(1)}) custom-call(bf16[2,1280,64]{2,1,0:T(8,128)(2,1)S(1)} %bitcast.60, bf16[128,64]{1,0:T(8,128)(2,1)S(1)} %bitcast.67, bf16[16,32]{1,0:T(8,128)(2,1)S(1)} %bitcast.68, ...), custom_call_target="tpu_custom_call" | custom-call | flops 67108864 | bytes 1048576 | tf_op jit(solution)/shard_map/pallas_call | solution.py:26
  12.0 0.0 copy-done
  12.0 1.1 %fusion.8.part_ref = bf16[16,64,128]{2,1,0:T(8,128)(2,1)S(1)} fusion(bf16[64,32,8,16,1]{0,3,2,1,4:T(8,128)(2,1)S(1)} %bitcast.62, bf16[8,128,32,8]{1,3,2,0:T(8,128)(2,1)S(1)} %copy-done, bf16[8,64,64]{2,1,0:T(8,128)(2,1)S(1)} %get-tuple-element.16), kind=kOutput, calls=%fused_computation.5 | convolution fusion | flops 672268288 | bytes 1376256 | tf_op jit(solution)/shard_map/cxa,cxib->aib/dot_general | solution.py:238
  13.2 0.3 shard_map.88
  13.4 0.0 copy-start.1
  13.4 2.1 %all-gather.1 = bf16[8,128,128]{2,1,0:T(8,128)(2,1)S(1)} all-gather(bf16[4,128,128]{2,1,0:T(8,128)(2,1)S(1)} %get-tuple-element.19), channel_id=3, replica_groups=mesh['sys'=32,'mode'=8,'rank'=2] {'rank'}, dimensions={0}, use_global_device_ids=true | all-gather | bytes 393216 | tf_op jit(solution)/shard_map/all_gather | solution.py:244
  15.6 10.7 %all_to_all.10.recv_ref = bf16[8,224,128]{2,1,0:T(8,128)(2,1)S(1)} all-to-all(bf16[8,224,128]{2,1,0:T(8,128)(2,1)S(1)} %shard_map.89), channel_id=1, replica_groups=mesh['sys'=32,'mode'=8,'rank'=2] {'mode'}, dimensions={0} | all-to-all | bytes 917504 | tf_op jit(solution)/shard_map/all_to_all | solution.py:254
  26.3 0.0 copy-done.1
  26.3 1.2 %shard_map.90 = (f32[16,1024]{1,0:T(8,128)S(1)}, f32[16,16,128]{2,1,0:T(8,128)}, f32[64,64]{1,0:T(8,128)S(1)}) custom-call(bf16[8,224,128]{2,1,0:T(8,128)(2,1)S(1)} %all_to_all.10.recv_ref, f32[512,32]{1,0:T(8,128)S(1)} %get-tuple-element.21.rhs_ref, bf16[1024,64]{1,0:T(8,128)(2,1)S(1)} %bitcast.64), custom_call_target="tpu_custom_call" | custom-call | flops 16777216 | bytes 1048576 | tf_op jit(solution)/shard_map/pallas_call | solution.py:26
  27.6 5.3 %all-to-all-start.1 = ((f32[16,16,128]{2,1,0:T(8,128)}), f32[16,16,128]{2,1,0:T(8,128)S(1)}, u32[]{:S(2)}, u32[]{:S(2)}) async-start(f32[16,16,128]{2,1,0:T(8,128)} %get-tuple-element.22), calls=%async_computation.1 | async-start | bytes 262144 | tf_op jit(solution)/shard_map/all_to_all | solution.py:264
  32.9 5.7 %shard_map.91 = (f32[64,128]{1,0:T(8,128)S(1)}, f32[64,1024]{1,0:T(8,128)S(1)}, bf16[256,1024]{1,0:T(8,128)(2,1)S(1)}) custom-call(f32[64,64]{1,0:T(8,128)S(1)} %get-tuple-element.23.gram_ref, bf16[1024,64]{1,0:T(8,128)(2,1)S(1)} %bitcast.65), custom_call_target="tpu_custom_call" | custom-call | flops 4294967296 | bytes 1048576 | tf_op jit(solution)/shard_map/pallas_call | solution.py:26
  38.6 0.5 %all-to-all-done.1.recv_ref = f32[16,16,128]{2,1,0:T(8,128)S(1)} async-done(((f32[16,16,128]{2,1,0:T(8,128)}), f32[16,16,128]{2,1,0:T(8,128)S(1)}, u32[]{:S(2)}, u32[]{:S(2)}) %all-to-all-start.1) | async-done | bytes 131104 | tf_op jit(solution)/shard_map/all_to_all | solution.py:264
  39.1 1.8 %shard_map.92 = (f32[1024,80]{1,0:T(8,128)}, f32[80,80]{1,0:T(8,128)}) custom-call(f32[16,16,128]{2,1,0:T(8,128)S(1)} %all-to-all-done.1.recv_ref, f32[64,128]{1,0:T(8,128)S(1)} %get-tuple-element.24.both_ref, f32[64,1024]{1,0:T(8,128)S(1)} %get-tuple-element.25.ortho_ref, bf16[256,1024]{1,0:T(8,128)(2,1)S(1)} %get-tuple-element.26.parts_ref, ...), custom_call_target="tpu_custom_call" | custom-call | flops 67108864 | bytes 1048576 | tf_op jit(solution)/shard_map/pallas_call | solution.py:26
  (1 shorter events, 0.0 us)
Async XLA Ops:
  0.6 11.4 %copy-start = (bf16[8,128,32,8]{1,3,2,0:T(8,128)(2,1)S(1)}, bf16[8,128,32,8]{1,3,2,0:T(8,128)(2,1)}, u32[]{:S(2)}) copy-start(bf16[8,128,32,8]{1,3,2,0:T(8,128)(2,1)} %param.8) | copy-start | bytes 1572868
  0.6 9.8 %copy-start.3 = (bf16[64,8,16]{0,2,1:T(8,128)(2,1)S(1)}, bf16[64,8,16]{0,2,1:T(8,128)(2,1)}, u32[]{:S(2)}) copy-start(bf16[64,8,16]{0,2,1:T(8,128)(2,1)} %param.10) | copy-start | bytes 49156
  0.7 9.8 %copy-start.4 = (bf16[32,16]{0,1:T(8,128)(2,1)S(1)}, bf16[32,16]{0,1:T(8,128)(2,1)}, u32[]{:S(2)}) copy-start(bf16[32,16]{0,1:T(8,128)(2,1)} %param.11) | copy-start | bytes 3076
  0.7 9.8 %copy-start.2 = (bf16[16,32,16]{1,2,0:T(8,128)(2,1)S(1)}, bf16[16,32,16]{1,2,0:T(8,128)(2,1)}, u32[]{:S(2)}) copy-start(bf16[16,32,16]{1,2,0:T(8,128)(2,1)} %param.12) | copy-start | bytes 49156
  0.7 9.8 %copy-start.5 = (bf16[16,16]{1,0:T(8,128)(2,1)S(1)}, bf16[16,16]{1,0:T(8,128)(2,1)}, u32[]{:S(2)}) copy-start(bf16[16,16]{1,0:T(8,128)(2,1)} %rhs_right_ref.1) | copy-start | bytes 1540
  13.4 12.9 %copy-start.1 = (bf16[32,32,64]{2,1,0:T(8,128)(2,1)S(1)}, bf16[32,32,64]{2,1,0:T(8,128)(2,1)}, u32[]{:S(2)}) copy-start(bf16[32,32,64]{2,1,0:T(8,128)(2,1)} %param.7) | copy-start | bytes 393220
  27.6 11.5 %all-to-all-start.1 = ((f32[16,16,128]{2,1,0:T(8,128)}), f32[16,16,128]{2,1,0:T(8,128)S(1)}, u32[]{:S(2)}, u32[]{:S(2)}) async-start(f32[16,16,128]{2,1,0:T(8,128)} %get-tuple-element.22), calls=%async_computation.1 | async-start | bytes 262144 | tf_op jit(solution)/shard_map/all_to_all | solution.py:264

commit v4 on v3

--- a/solution.py
+++ b/solution.py
@@ -14,6 +14,7 @@
 RZ = 16
 RA = 8
 HALF = 32
+PITCH = 33
 ROWS = 1024
 NT = (((1,), (1,)), ((), ()))
 TN = (((0,), (0,)), ((), ()))
@@ -57,18 +58,13 @@
         copy.wait()
 
 
-def same(rows, lanes, row_of, lane_of):
-    row = lax.broadcasted_iota(jnp.int32, (rows, lanes), 0)
-    lane = lax.broadcasted_iota(jnp.int32, (rows, lanes), 1)
-    return row_of(row) == lane_of(lane)
-
-
-def project(both_ref, right_ref, rhs_left_ref, rhs_core_ref, rhs_right_ref, proj_ref, left_ref, gram_ref, rhs_ref, sol_ref):
-    sol_ref[0:ROWS] = both_ref[0, 0:ROWS].astype(F32)
-    sol_ref[ROWS : 2 * ROWS] = both_ref[1, 0:ROWS].astype(F32)
+def project(rank_ref, both_ref, right_ref, rhs_left_ref, rhs_core_ref, rhs_right_ref, proj_ref, left_ref, gram_ref, rhs_ref, sol_ref):
+    for c in range(R):
+        own = HALF * (c % HALF)
+        sol_ref[PITCH * c : PITCH * c + 32] = both_ref[c // HALF, own : own + 32].astype(F32)
     right = right_ref[...]
     for j in range(32):
-        rows = sol_ref[pl.ds(j, R, stride=32), :].astype(BF16)
+        rows = sol_ref[pl.ds(j, R, stride=PITCH), :].astype(BF16)
         proj_ref[j] = lax.dot_general(right, rows, NT, preferred_element_type=F32).astype(BF16)
     for x in range(RA):
         for r in range(2):
@@ -77,27 +73,31 @@
     for r in range(2):
         s = both_ref[r, 0:ROWS]
         gram = gram + lax.dot_general(s, s, TN, preferred_element_type=F32)
-    for p, part in enumerate(three_parts(gram)):
-        part = part.astype(F32)
-        gram_ref[HALF * p : HALF * (p + 1)] = jnp.concatenate([part[:HALF], part[HALF:]], axis=1).astype(BF16)
-    group = lax.broadcasted_iota(jnp.int32, (HALF, 128), 1) >> 4
+    row = lax.broadcasted_iota(jnp.int32, (HALF, HALF), 0)
+    lane = lax.broadcasted_iota(jnp.int32, (HALF, HALF), 1)
+    corner = gram[HALF:, HALF:]
+    half = jnp.where(rank_ref[0] == 0, jnp.where(row >= lane, gram[:HALF, :HALF], corner), gram[HALF:, :HALF])
+    half = jnp.concatenate([half[8 * k : 8 * (k + 1)] for k in range(4)], axis=1)
+    diagonal = jnp.sum(jnp.where(row == lane, corner, 0.0), axis=0, keepdims=True)
+    diagonal = jnp.broadcast_to(jnp.concatenate([diagonal] * 4, axis=1), (8, 128))
+    row = lax.broadcasted_iota(jnp.int32, (8, 128), 0)
+    parts = [part.astype(F32) for part in three_parts(half)]
+    tail = jnp.zeros((8, 128), F32)
+    for p, part in enumerate(three_parts(diagonal)):
+        tail = jnp.where(row == p, part.astype(F32), tail)
+    gram_ref[...] = jnp.concatenate([*parts, tail], axis=0).astype(BF16)
     turned = jnp.concatenate([rhs_right_ref[...].astype(F32).T] * 8, axis=1)
     turned = jnp.broadcast_to(turned[:, None, :], (16, 16, 128)).reshape(256, 128)
     row = lax.broadcasted_iota(jnp.int32, (256, 128), 0) & 15
     lane = lax.broadcasted_iota(jnp.int32, (256, 128), 1) >> 4
     spread = jnp.concatenate([jnp.where(row == lane + 8 * h, turned, 0.0) for h in range(2)], axis=1).astype(BF16)
-    half_done = jnp.dot(spread, rhs_core_ref[...], preferred_element_type=F32)
-    turned = jnp.concatenate([rhs_left_ref[...].astype(F32).T] * 8, axis=1)
-    blank = jnp.zeros((HALF, 128), F32)
-    spread = []
-    for b in range(RZ):
-        tile = jnp.where(group == b % 8, turned, 0.0)
-        spread.append(jnp.concatenate([tile, blank] if b < 8 else [blank, tile], axis=1))
-    spread = jnp.concatenate(spread, axis=0).astype(BF16)
-    total = jnp.zeros((512, 32), F32)
-    for part in three_parts(half_done):
-        total = total + jnp.dot(spread, part, preferred_element_type=F32)
-    rhs_ref[...] = total
+    inner = jnp.dot(spread, rhs_core_ref[...], preferred_element_type=F32)
+    inner = jnp.concatenate([inner[RZ * b : RZ * (b + 1)] for b in range(RZ)], axis=1)
+    stacked = jnp.concatenate(three_parts(inner), axis=0)
+    outer = rhs_left_ref[...].astype(F32).T.astype(BF16)
+    total = jnp.dot(jnp.concatenate([outer] * 3, axis=1), stacked, preferred_element_type=F32)
+    for g in range(4):
+        rhs_ref[HALF * g : HALF * (g + 1)] = total[:, 128 * g : 128 * (g + 1)]
 
 
 def pack(rank_ref, part_ref, keep_ref, give_ref):
@@ -118,23 +118,23 @@
         out_ref[4 * rank + q, 0:128] = keep_ref[q]
         out_ref[4 - 4 * rank + q, 0:128] = every_ref[1 - rank, q]
     for k in range(8):
-        out_ref[k, 128:224] = gram
+        out_ref[k, 128:160] = gram
 
 
 def residual(recv_ref, rhs_ref, sol_ref, turned_ref, send_ref, gram_ref, rows_ref):
     total = recv_ref[0].astype(F32)
     for m in range(1, 8):
         total = total + recv_ref[m].astype(F32)
-    packed = total[128:160] + total[160:192] + total[192:224]
-    gram_ref[0:HALF] = packed[:, 0:R]
-    gram_ref[HALF:R] = packed[:, R:]
+    gram_ref[0:8] = total[128:136] + total[136:144] + total[144:152]
+    gram_ref[8:16] = jnp.broadcast_to(total[152:153] + total[153:154] + total[154:155], (8, 128))
+    resid = rhs_ref[...] - total[0:128]
     for k in range(4):
-        shifted = total[0:128] if k == 0 else pltpu.roll(total[0:128], 128 - 32 * k, 1)
+        shifted = resid if k == 0 else pltpu.roll(resid, 128 - 32 * k, 1)
         for g in range(4):
-            rows = slice(HALF * (4 * g + k), HALF * (4 * g + k + 1))
-            rows_ref[rows] = rhs_ref[rows] - shifted[HALF * g : HALF * (g + 1), :32]
+            b = 4 * g + k
+            rows_ref[PITCH * b : PITCH * b + HALF] = shifted[HALF * g : HALF * (g + 1), :32]
     for t in range(8):
-        four = [rows_ref[pl.ds(4 * t + s, RZ, stride=32), :] for s in range(4)]
+        four = [rows_ref[pl.ds(4 * t + s, RZ, stride=PITCH), :] for s in range(4)]
         turned_ref[:, 128 * t : 128 * (t + 1)] = jnp.concatenate(four, axis=1)
     turned = turned_ref[...]
     stacked = jnp.concatenate(three_parts(turned), axis=0)
@@ -146,20 +146,41 @@
         send_ref[k] = row
 
 
-def eliminate(m, n):
-    index = lax.broadcasted_iota(jnp.int32, (n, 1), 0)
-    for k in range(n):
-        row = m[k : k + 1]
-        factor = jnp.where(index > k, m[:, k : k + 1] / m[k : k + 1, k : k + 1], 0.0)
-        m = m - factor * row
-    lane = lax.broadcasted_iota(jnp.int32, m.shape, 1)
-    pivot = jnp.sum(jnp.where(lane == index, m, 0.0), axis=1, keepdims=True)
-    return m * lax.rsqrt(pivot)
+def eliminate(square, blocks):
+    columns = [jnp.broadcast_to(square[:, k : k + 1], (RZ, 128)) for k in range(RZ)]
+    index = lax.broadcasted_iota(jnp.int32, (RZ, 128), 0)
+    pivots = jnp.zeros((RZ, 128), F32)
+    for k in range(RZ):
+        pivots = jnp.where(index == k, columns[k], pivots)
+        factor = jnp.where(index > k, columns[k] / columns[k][k : k + 1], 0.0)
+        for j in range(k + 1, RZ):
+            columns[j] = columns[j] - factor * columns[j][k : k + 1]
+        blocks = [x - factor * x[k : k + 1] for x in blocks]
+    return lax.rsqrt(pivots), columns, blocks
 
 
 def first_block(gram_ref, sol_ref, both_ref, ortho_ref, parts_ref):
-    eye = same(R, R, lambda r: r, lambda l: l).astype(F32)
-    both = eliminate(jnp.concatenate([gram_ref[...], eye], axis=1), R)
+    row = lax.broadcasted_iota(jnp.int32, (HALF, HALF), 0)
+    lane = lax.broadcasted_iota(jnp.int32, (HALF, HALF), 1)
+    halves = [jnp.concatenate([gram_ref[r, 0:8, 32 * k : 32 * (k + 1)] for k in range(4)], axis=0) for r in range(2)]
+    mirror = halves[0].T
+    first = jnp.where(row >= lane, halves[0], mirror)
+    corner = jnp.where(row < lane, halves[0], mirror)
+    corner = jnp.where(row == lane, gram_ref[0, 8:9, 0:32], corner)
+    eye = (lax.broadcasted_iota(jnp.int32, (R, R), 0) == lax.broadcasted_iota(jnp.int32, (R, R), 1)).astype(F32)
+    gram = jnp.concatenate(
+        [jnp.concatenate([first, halves[1].T], axis=1), jnp.concatenate([halves[1], corner], axis=1)], axis=0
+    )
+    rest = jnp.concatenate([gram, eye], axis=1)
+    done = []
+    for k in range(4):
+        scale, _, (top,) = eliminate(rest[0:RZ, RZ * k : RZ * (k + 1)], [rest[0:RZ]])
+        top = top * scale
+        done.append(top)
+        if k < 3:
+            across = top[:, RZ * (k + 1) : R]
+            rest = rest[RZ:] - lax.dot_general(across, top, TN, precision=HIGHEST, preferred_element_type=F32)
+    both = jnp.concatenate(done, axis=0)
     both_ref[...] = both
     stacked = jnp.concatenate(three_parts(both[:, R:]), axis=0)
     ortho = lax.dot_general(stacked, sol_ref[...], NT, preferred_element_type=F32)
@@ -181,23 +202,18 @@
     wide = jnp.concatenate([hi, hi, mid, mid], axis=1)
     resid = turned_ref[...] - jnp.dot(wide, parts_ref[...], preferred_element_type=F32)
     blocks = [resid[:, 128 * t : 128 * (t + 1)] for t in range(8)]
-    columns = [jnp.broadcast_to(schur[:, k : k + 1], (RZ, 128)) for k in range(RZ)]
+    scale, columns, blocks = eliminate(schur, blocks)
     index = lax.broadcasted_iota(jnp.int32, (RZ, 128), 0)
     lane = lax.broadcasted_iota(jnp.int32, (RZ, 128), 1)
-    pivots = jnp.zeros((RZ, 128), F32)
     upper = jnp.zeros((RZ, 128), F32)
     for k in range(RZ):
-        pivots = jnp.where(index == k, columns[k], pivots)
         upper = jnp.where((lane == R + k) & (index <= k), columns[k], upper)
-        factor = jnp.where(index > k, columns[k] / columns[k][k : k + 1], 0.0)
-        for j in range(k + 1, RZ):
-            columns[j] = columns[j] - factor * columns[j][k : k + 1]
-        blocks = [x - factor * x[k : k + 1] for x in blocks]
-    scale = lax.rsqrt(pivots)
     for t in range(8):
-        lanes = slice(128 * t, 128 * (t + 1))
-        q_ref[lanes] = jnp.concatenate([ortho_ref[:, lanes], blocks[t] * scale], axis=0).T
-    r_ref[0:R] = jnp.concatenate([both[:, :R], cross.T], axis=1)
+        rows = slice(128 * t, 128 * (t + 1))
+        q_ref[rows] = jnp.concatenate([ortho_ref[:, rows], blocks[t] * scale], axis=0).T
+    row = lax.broadcasted_iota(jnp.int32, (R, R), 0)
+    lane = lax.broadcasted_iota(jnp.int32, (R, R), 1)
+    r_ref[0:R] = jnp.concatenate([jnp.where(row <= lane, both[:, :R], 0.0), cross.T], axis=1)
     r_ref[R:] = (upper * scale)[:, : R + RZ]
 
 
@@ -216,35 +232,37 @@
     )
     both = lax.all_gather(own, "rank", axis=0)
     right = jnp.transpose(right_interface, (1, 2, 0)).reshape(RA * RZ, R)
+    rank = lax.axis_index("rank").astype(jnp.int32).reshape(1)
+    smem = pl.BlockSpec(memory_space=pltpu.SMEM)
     proj, left, early, rhs_term = call(
         project,
         (
             shape((32, 128, R), BF16),
             shape((RA, R, R), BF16),
-            shape((96, 128), BF16),
-            shape((512, 32), F32),
+            shape((32, 128), BF16),
+            shape((128, 128), F32),
         ),
+        rank,
         both,
         right,
         rhs_left.T,
         jnp.transpose(rhs_core, (0, 2, 1)).reshape(256, 32),
         rhs_right,
-        scratch=[pltpu.VMEM((2 * ROWS, R), F32)],
+        scratch=[pltpu.VMEM((R * PITCH, R), F32)],
         flops=1 << 26,
+        in_specs=[smem] + [VMEM] * 5,
     )
     proj = jnp.transpose(proj.reshape(32, RA, RZ, R), (3, 0, 1, 2))
     left = jnp.transpose(left, (1, 0, 2))
     applied = jnp.einsum("xijy,cjyb->cxib", operator_core, proj, preferred_element_type=F32).astype(BF16)
     partial_value = jnp.einsum("cxa,cxib->aib", left, applied, preferred_element_type=F32)
     partial_value = jnp.transpose(partial_value, (2, 0, 1)).astype(BF16)
-    rank = lax.axis_index("rank").astype(jnp.int32).reshape(1)
-    smem = pl.BlockSpec(memory_space=pltpu.SMEM)
     chunks = shape((4, 128, 128), BF16)
     keep, give = call(pack, (chunks, chunks), rank, partial_value, flops=1 << 24, in_specs=[smem, VMEM])
     everyone = lax.all_gather(give, "rank", axis=0)
     send = call(
         choose,
-        shape((8, 224, 128), BF16),
+        shape((8, 160, 128), BF16),
         rank,
         keep,
         everyone,
@@ -254,14 +272,15 @@
     recv = lax.all_to_all(send, "mode", split_axis=0, concat_axis=0, tiled=True)
     turned, send, gram = call(
         residual,
-        (shape((RZ, ROWS), F32), shape((16, RZ, 128), F32), shape((R, R), F32)),
+        (shape((RZ, ROWS), F32), shape((16, RZ, 128), F32), shape((16, 128), F32)),
         recv,
         rhs_term,
         sol,
-        scratch=[pltpu.VMEM((512, 32), F32)],
+        scratch=[pltpu.VMEM((RZ * PITCH, 32), F32)],
         flops=1 << 24,
     )
     recv = lax.all_to_all(send, ("mode", "rank"), split_axis=0, concat_axis=0, tiled=True)
+    gram = lax.all_gather(gram, "rank", axis=0)
     factor, ortho, parts = call(
         first_block,
         (shape((R, 2 * R), F32), shape((R, ROWS), F32), shape((4 * R, ROWS), BF16)),

time: 41.2 us -> 39 us (0.947)
  Pallas kernels: 11.6 us -> 7.72 us
  waiting for transfers between devices: 0.49 us -> 1.83 us
  blocking collectives: 21.6 us -> 22.5 us
  starting transfers between devices: 5.34 us -> 4.81 us
    pallas_call x7, Pallas kernels: 11.6 us -> 7.72 us  [call(): pl.pallas_call(body, out_shape=outs, in_specs=in_specs or [VMEM] * len(ar...]
    all_gather x0 -> x1, blocking collectives: none -> 1.81 us  [per_device(): gram = lax.all_gather(gram, 'rank', axis=0)]
    all_to_all x1, waiting for transfers between devices: 0.49 us -> 1.83 us  [per_device(): lax.all_to_all(send, ('mode', 'rank'), split_axis=0, concat_axis=0, tiled...]
    all_to_all x1, blocking collectives: 10.7 us -> 9.93 us  [per_device(): recv = lax.all_to_all(send, 'mode', split_axis=0, concat_axis=0, tiled=True)]
    all_to_all x1, starting transfers between devices: 5.34 us -> 4.81 us  [per_device(): lax.all_to_all(send, ('mode', 'rank'), split_axis=0, concat_axis=0, tiled...]
  transfers between devices with their start and end apart: 1 -> 1, of which waited for: 1 -> 1; matrix products, arithmetic and copies ran while one was open for 0% -> 0% of each run, Pallas kernels for 14% -> 7%
where the time goes in v4:
time: 39 us; the launch traced here: 38.7 us
  blocking collectives  22.5 us (58%)
  Pallas kernels  7.72 us (20%)
  starting transfers between devices  4.81 us (12%)
  waiting for transfers between devices  1.83 us (5%)
  matrix products  1.1 us (3%)
  between operations  0.74 us (2%)
    all_to_all x1, blocking collectives, per_device(): recv = lax.all_to_all(send, 'mode', split_axis=0, concat_axis=0, tiled=True)  9.93 us
    all_gather x1, blocking collectives, per_device(): both = lax.all_gather(own, 'rank', axis=0)  8.74 us
    pallas_call x7, Pallas kernels, call(): pl.pallas_call(body, out_shape=outs, in_specs=in_specs or [VMEM] * len(ar...  7.72 us
    all_to_all x1, starting transfers between devices, per_device(): lax.all_to_all(send, ('mode', 'rank'), split_axis=0, concat_axis=0, tiled...  4.81 us
    all_gather x1, blocking collectives, per_device(): everyone = lax.all_gather(give, 'rank', axis=0)  2.01 us
    all_to_all x1, waiting for transfers between devices, per_device(): lax.all_to_all(send, ('mode', 'rank'), split_axis=0, concat_axis=0, tiled...  1.83 us
    all_gather x1, blocking collectives, per_device(): gram = lax.all_gather(gram, 'rank', axis=0)  1.81 us
    dot_general x1, matrix products, per_device(): jnp.einsum('cxa,cxib->aib', left, applied, preferred_element_type=F32)  1.1 us
  transfers between devices with their start and end apart: 1, of which 1 were waited for; matrix products, arithmetic and copies ran while one was open for 0% of the time, Pallas kernels for 7%

profile of v4, /device:TPU:1, one launch (start us, length us, event | category | flops | bytes accessed | tf_op | source)
XLA Modules:
  0.0 38.7 jit_solution(693202104799152373)
XLA Ops:
  0.6 0.0 copy-start
  0.6 0.0 copy-start.5
  0.7 0.0 copy-start.2
  0.7 0.0 copy-start.4
  0.7 0.0 copy-start.3
  0.7 1.0 %shard_map.86 = bf16[1280,64]{1,0:T(8,128)(2,1)S(1)} custom-call(bf16[1024,64]{1,0:T(8,128)(2,1)} %bitcast.62, bf16[256,64]{1,0:T(8,128)(2,1)} %bitcast.71), custom_call_target="tpu_custom_call" | custom-call | bytes 1048576 | tf_op jit(solution)/shard_map/pallas_call | solution.py:27
  1.7 8.7 %all-gather = bf16[2560,64]{1,0:T(8,128)(2,1)S(1)} all-gather(bf16[1280,64]{1,0:T(8,128)(2,1)S(1)} %shard_map.86), channel_id=2, replica_groups=mesh['sys'=32,'mode'=8,'rank'=2] {'rank'}, dimensions={0}, use_global_device_ids=true | all-gather | bytes 491520 | tf_op jit(solution)/shard_map/all_gather | solution.py:233
  10.5 0.0 copy-done.5
  10.5 0.0 copy-done.2
  10.5 0.0 copy-done.4
  10.5 0.0 copy-done.3
  10.5 0.8 %shard_map.87 = (bf16[32,128,64]{2,1,0:T(8,128)(2,1)S(1)}, bf16[8,64,64]{2,1,0:T(8,128)(2,1)S(1)}, bf16[32,128]{1,0:T(8,128)(2,1)S(1)}, f32[128,128]{1,0:T(8,128)S(1)}) custom-call(s32[1]{0:T(128)} %bitcast.rank_ref, bf16[2,1280,64]{2,1,0:T(8,128)(2,1)S(1)} %bitcast.61, bf16[128,64]{1,0:T(8,128)(2,1)S(1)} %bitcast.68, bf16[16,32]{1,0:T(8,128)(2,1)S(1)} %bitcast.70, ...), custom_call_target="tpu_custom_call" | custom-call | flops 67108864 | bytes 1048576 | tf_op jit(solution)/shard_map/pallas_call | solution.py:27
  11.3 0.0 copy-done
  11.3 1.1 %fusion.8.part_ref = bf16[16,64,128]{2,1,0:T(8,128)(2,1)S(1)} fusion(bf16[64,32,8,16,1]{0,3,2,1,4:T(8,128)(2,1)S(1)} %bitcast.66, bf16[8,128,32,8]{1,3,2,0:T(8,128)(2,1)S(1)} %copy-done, bf16[8,64,64]{2,1,0:T(8,128)(2,1)S(1)} %get-tuple-element.16), kind=kOutput, calls=%fused_computation.5 | convolution fusion | flops 672268288 | bytes 1376256 | tf_op jit(solution)/shard_map/cxa,cxib->aib/dot_general | solution.py:258
  12.4 0.0 copy-start.1
  12.4 0.3 shard_map.88
  12.7 2.0 %all-gather.1 = bf16[8,128,128]{2,1,0:T(8,128)(2,1)S(1)} all-gather(bf16[4,128,128]{2,1,0:T(8,128)(2,1)S(1)} %get-tuple-element.19), channel_id=3, replica_groups=mesh['sys'=32,'mode'=8,'rank'=2] {'rank'}, dimensions={0}, use_global_device_ids=true | all-gather | bytes 393216 | tf_op jit(solution)/shard_map/all_gather | solution.py:262
  14.8 9.9 %all_to_all.10.recv_ref = bf16[8,160,128]{2,1,0:T(8,128)(2,1)S(1)} all-to-all(bf16[8,160,128]{2,1,0:T(8,128)(2,1)S(1)} %shard_map.89), channel_id=1, replica_groups=mesh['sys'=32,'mode'=8,'rank'=2] {'mode'}, dimensions={0} | all-to-all | bytes 655360 | tf_op jit(solution)/shard_map/all_to_all | solution.py:272
  24.7 1.2 %shard_map.90 = (f32[16,1024]{1,0:T(8,128)S(1)}, f32[16,16,128]{2,1,0:T(8,128)}, f32[16,128]{1,0:T(8,128)S(1)}) custom-call(bf16[8,160,128]{2,1,0:T(8,128)(2,1)S(1)} %all_to_all.10.recv_ref, f32[128,128]{1,0:T(8,128)S(1)} %get-tuple-element.21.rhs_ref, bf16[1024,64]{1,0:T(8,128)(2,1)S(1)} %bitcast.63), custom_call_target="tpu_custom_call" | custom-call | flops 16777216 | bytes 1048576 | tf_op jit(solution)/shard_map/pallas_call | solution.py:27
  25.9 4.8 %all-to-all-start.1 = ((f32[16,16,128]{2,1,0:T(8,128)}), f32[16,16,128]{2,1,0:T(8,128)S(1)}, u32[]{:S(2)}, u32[]{:S(2)}) async-start(f32[16,16,128]{2,1,0:T(8,128)} %get-tuple-element.22), calls=%async_computation.1 | async-start | bytes 262144 | tf_op jit(solution)/shard_map/all_to_all | solution.py:282
  30.7 1.8 %all-gather.2 = f32[32,128]{1,0:T(8,128)S(1)} all-gather(f32[16,128]{1,0:T(8,128)S(1)} %get-tuple-element.23), channel_id=4, replica_groups=mesh['sys'=32,'mode'=8,'rank'=2] {'rank'}, dimensions={0}, use_global_device_ids=true | all-gather | bytes 24576 | tf_op jit(solution)/shard_map/all_gather | solution.py:283
  32.5 2.6 %shard_map.91 = (f32[64,128]{1,0:T(8,128)S(1)}, f32[64,1024]{1,0:T(8,128)S(1)}, bf16[256,1024]{1,0:T(8,128)(2,1)S(1)}) custom-call(f32[2,16,128]{2,1,0:T(8,128)S(1)} %bitcast.69, bf16[1024,64]{1,0:T(8,128)(2,1)S(1)} %bitcast.64), custom_call_target="tpu_custom_call" | custom-call | flops 4294967296 | bytes 1048576 | tf_op jit(solution)/shard_map/pallas_call | solution.py:27
  35.1 1.8 %all-to-all-done.1.recv_ref = f32[16,16,128]{2,1,0:T(8,128)S(1)} async-done(((f32[16,16,128]{2,1,0:T(8,128)}), f32[16,16,128]{2,1,0:T(8,128)S(1)}, u32[]{:S(2)}, u32[]{:S(2)}) %all-to-all-start.1) | async-done | bytes 131104 | tf_op jit(solution)/shard_map/all_to_all | solution.py:282
  36.9 1.8 %shard_map.92 = (f32[1024,80]{1,0:T(8,128)}, f32[80,80]{1,0:T(8,128)}) custom-call(f32[16,16,128]{2,1,0:T(8,128)S(1)} %all-to-all-done.1.recv_ref, f32[64,128]{1,0:T(8,128)S(1)} %get-tuple-element.24.both_ref, f32[64,1024]{1,0:T(8,128)S(1)} %get-tuple-element.25.ortho_ref, bf16[256,1024]{1,0:T(8,128)(2,1)S(1)} %get-tuple-element.26.parts_ref, ...), custom_call_target="tpu_custom_call" | custom-call | flops 67108864 | bytes 1048576 | tf_op jit(solution)/shard_map/pallas_call | solution.py:27
  (2 shorter events, 0.0 us)
Async XLA Ops:
  0.6 10.7 %copy-start = (bf16[8,128,32,8]{1,3,2,0:T(8,128)(2,1)S(1)}, bf16[8,128,32,8]{1,3,2,0:T(8,128)(2,1)}, u32[]{:S(2)}) copy-start(bf16[8,128,32,8]{1,3,2,0:T(8,128)(2,1)} %param.8) | copy-start | bytes 1572868
  0.6 9.8 %copy-start.5 = (bf16[16,16]{1,0:T(8,128)(2,1)S(1)}, bf16[16,16]{1,0:T(8,128)(2,1)}, u32[]{:S(2)}) copy-start(bf16[16,16]{1,0:T(8,128)(2,1)} %rhs_right_ref.1) | copy-start | bytes 1540
  0.7 9.8 %copy-start.2 = (bf16[16,32,16]{1,2,0:T(8,128)(2,1)S(1)}, bf16[16,32,16]{1,2,0:T(8,128)(2,1)}, u32[]{:S(2)}) copy-start(bf16[16,32,16]{1,2,0:T(8,128)(2,1)} %param.12) | copy-start | bytes 49156
  0.7 9.8 %copy-start.4 = (bf16[32,16]{0,1:T(8,128)(2,1)S(1)}, bf16[32,16]{0,1:T(8,128)(2,1)}, u32[]{:S(2)}) copy-start(bf16[32,16]{0,1:T(8,128)(2,1)} %param.11) | copy-start | bytes 3076
  0.7 9.8 %copy-start.3 = (bf16[64,8,16]{0,2,1:T(8,128)(2,1)S(1)}, bf16[64,8,16]{0,2,1:T(8,128)(2,1)}, u32[]{:S(2)}) copy-start(bf16[64,8,16]{0,2,1:T(8,128)(2,1)} %param.10) | copy-start | bytes 49156
  12.4 12.3 %copy-start.1 = (bf16[32,32,64]{2,1,0:T(8,128)(2,1)S(1)}, bf16[32,32,64]{2,1,0:T(8,128)(2,1)}, u32[]{:S(2)}) copy-start(bf16[32,32,64]{2,1,0:T(8,128)(2,1)} %param.7) | copy-start | bytes 393220
  25.9 11.0 %all-to-all-start.1 = ((f32[16,16,128]{2,1,0:T(8,128)}), f32[16,16,128]{2,1,0:T(8,128)S(1)}, u32[]{:S(2)}, u32[]{:S(2)}) async-start(f32[16,16,128]{2,1,0:T(8,128)} %get-tuple-element.22), calls=%async_computation.1 | async-start | bytes 262144 | tf_op jit(solution)/shard_map/all_to_all | solution.py:282

commit v5 on v4

--- a/solution.py
+++ b/solution.py
@@ -140,7 +140,9 @@
     stacked = jnp.concatenate(three_parts(turned), axis=0)
     cross = jnp.dot(stacked, sol_ref[...], preferred_element_type=F32)
     cross = cross[0:16] + cross[16:32] + cross[32:48]
-    own = lax.dot_general(turned, turned, NT, precision=HIGHEST, preferred_element_type=F32)
+    pairs = lax.dot_general(stacked, stacked, NT, preferred_element_type=F32)
+    own = pairs[0:16, 16:32] + pairs[0:16, 32:48] + pairs[16:32, 16:32] + pairs[16:32, 0:16] + pairs[32:48, 0:16]
+    own = own + pairs[0:16, 0:16]
     row = jnp.concatenate([cross, own, jnp.zeros((RZ, 48), F32)], axis=1)
     for k in range(16):
         send_ref[k] = row
@@ -248,7 +250,7 @@
         rhs_left.T,
         jnp.transpose(rhs_core, (0, 2, 1)).reshape(256, 32),
         rhs_right,
-        scratch=[pltpu.VMEM((R * PITCH, R), F32)],
+        scratch=[pltpu.VMEM(((R + 1) * PITCH, R), F32)],
         flops=1 << 26,
         in_specs=[smem] + [VMEM] * 5,
     )
@@ -276,7 +278,7 @@
         recv,
         rhs_term,
         sol,
-        scratch=[pltpu.VMEM((RZ * PITCH, 32), F32)],
+        scratch=[pltpu.VMEM(((RZ + 1) * PITCH, 32), F32)],
         flops=1 << 24,
     )
     recv = lax.all_to_all(send, ("mode", "rank"), split_axis=0, concat_axis=0, tiled=True)

time: 39 us -> 38.9 us (level)
  no operation moved by 1% of the time
where the time goes in v5:
time: 38.9 us; the launch traced here: 38.7 us
  blocking collectives  22.5 us (58%)
  Pallas kernels  7.72 us (20%)
  starting transfers between devices  4.8 us (12%)
  waiting for transfers between devices  1.82 us (5%)
  matrix products  1.09 us (3%)
  between operations  0.74 us (2%)
    all_to_all x1, blocking collectives, per_device(): recv = lax.all_to_all(send, 'mode', split_axis=0, concat_axis=0, tiled=True)  9.93 us
    all_gather x1, blocking collectives, per_device(): both = lax.all_gather(own, 'rank', axis=0)  8.74 us
    pallas_call x7, Pallas kernels, call(): pl.pallas_call(body, out_shape=outs, in_specs=in_specs or [VMEM] * len(ar...  7.72 us
    all_to_all x1, starting transfers between devices, per_device(): lax.all_to_all(send, ('mode', 'rank'), split_axis=0, concat_axis=0, tiled...  4.8 us
    all_gather x1, blocking collectives, per_device(): everyone = lax.all_gather(give, 'rank', axis=0)  2.01 us
    all_to_all x1, waiting for transfers between devices, per_device(): lax.all_to_all(send, ('mode', 'rank'), split_axis=0, concat_axis=0, tiled...  1.82 us
    all_gather x1, blocking collectives, per_device(): gram = lax.all_gather(gram, 'rank', axis=0)  1.81 us
    dot_general x1, matrix products, per_device(): jnp.einsum('cxa,cxib->aib', left, applied, preferred_element_type=F32)  1.09 us
  transfers between devices with their start and end apart: 1, of which 1 were waited for; matrix products, arithmetic and copies ran while one was open for 0% of the time, Pallas kernels for 7%

profile of v5, /device:TPU:1, one launch (start us, length us, event | category | flops | bytes accessed | tf_op | source)
XLA Modules:
  0.0 38.7 jit_solution(17664961950618660233)
XLA Ops:
  0.6 0.0 copy-start
  0.6 0.0 copy-start.5
  0.7 0.0 copy-start.2
  0.7 0.0 copy-start.4
  0.7 0.0 copy-start.3
  0.7 1.0 %shard_map.86 = bf16[1280,64]{1,0:T(8,128)(2,1)S(1)} custom-call(bf16[1024,64]{1,0:T(8,128)(2,1)} %bitcast.62, bf16[256,64]{1,0:T(8,128)(2,1)} %bitcast.71), custom_call_target="tpu_custom_call" | custom-call | bytes 1048576 | tf_op jit(solution)/shard_map/pallas_call | solution.py:27
  1.7 8.7 %all-gather = bf16[2560,64]{1,0:T(8,128)(2,1)S(1)} all-gather(bf16[1280,64]{1,0:T(8,128)(2,1)S(1)} %shard_map.86), channel_id=2, replica_groups=mesh['sys'=32,'mode'=8,'rank'=2] {'rank'}, dimensions={0}, use_global_device_ids=true | all-gather | bytes 491520 | tf_op jit(solution)/shard_map/all_gather | solution.py:235
  10.5 0.0 copy-done.5
  10.5 0.0 copy-done.2
  10.5 0.0 copy-done.4
  10.5 0.0 copy-done.3
  10.5 0.8 %shard_map.87 = (bf16[32,128,64]{2,1,0:T(8,128)(2,1)S(1)}, bf16[8,64,64]{2,1,0:T(8,128)(2,1)S(1)}, bf16[32,128]{1,0:T(8,128)(2,1)S(1)}, f32[128,128]{1,0:T(8,128)S(1)}) custom-call(s32[1]{0:T(128)} %bitcast.rank_ref, bf16[2,1280,64]{2,1,0:T(8,128)(2,1)S(1)} %bitcast.61, bf16[128,64]{1,0:T(8,128)(2,1)S(1)} %bitcast.68, bf16[16,32]{1,0:T(8,128)(2,1)S(1)} %bitcast.70, ...), custom_call_target="tpu_custom_call" | custom-call | flops 67108864 | bytes 1048576 | tf_op jit(solution)/shard_map/pallas_call | solution.py:27
  11.3 0.0 copy-done
  11.3 1.1 %fusion.8.part_ref = bf16[16,64,128]{2,1,0:T(8,128)(2,1)S(1)} fusion(bf16[64,32,8,16,1]{0,3,2,1,4:T(8,128)(2,1)S(1)} %bitcast.66, bf16[8,128,32,8]{1,3,2,0:T(8,128)(2,1)S(1)} %copy-done, bf16[8,64,64]{2,1,0:T(8,128)(2,1)S(1)} %get-tuple-element.16), kind=kOutput, calls=%fused_computation.5 | convolution fusion | flops 672268288 | bytes 1376256 | tf_op jit(solution)/shard_map/cxa,cxib->aib/dot_general | solution.py:260
  12.4 0.0 copy-start.1
  12.4 0.3 shard_map.88
  12.7 2.0 %all-gather.1 = bf16[8,128,128]{2,1,0:T(8,128)(2,1)S(1)} all-gather(bf16[4,128,128]{2,1,0:T(8,128)(2,1)S(1)} %get-tuple-element.19), channel_id=3, replica_groups=mesh['sys'=32,'mode'=8,'rank'=2] {'rank'}, dimensions={0}, use_global_device_ids=true | all-gather | bytes 393216 | tf_op jit(solution)/shard_map/all_gather | solution.py:264
  14.8 9.9 %all_to_all.10.recv_ref = bf16[8,160,128]{2,1,0:T(8,128)(2,1)S(1)} all-to-all(bf16[8,160,128]{2,1,0:T(8,128)(2,1)S(1)} %shard_map.89), channel_id=1, replica_groups=mesh['sys'=32,'mode'=8,'rank'=2] {'mode'}, dimensions={0} | all-to-all | bytes 655360 | tf_op jit(solution)/shard_map/all_to_all | solution.py:274
  24.7 1.2 %shard_map.90 = (f32[16,1024]{1,0:T(8,128)S(1)}, f32[16,16,128]{2,1,0:T(8,128)}, f32[16,128]{1,0:T(8,128)S(1)}) custom-call(bf16[8,160,128]{2,1,0:T(8,128)(2,1)S(1)} %all_to_all.10.recv_ref, f32[128,128]{1,0:T(8,128)S(1)} %get-tuple-element.21.rhs_ref, bf16[1024,64]{1,0:T(8,128)(2,1)S(1)} %bitcast.63), custom_call_target="tpu_custom_call" | custom-call | flops 16777216 | bytes 1048576 | tf_op jit(solution)/shard_map/pallas_call | solution.py:27
  25.9 4.8 %all-to-all-start.1 = ((f32[16,16,128]{2,1,0:T(8,128)}), f32[16,16,128]{2,1,0:T(8,128)S(1)}, u32[]{:S(2)}, u32[]{:S(2)}) async-start(f32[16,16,128]{2,1,0:T(8,128)} %get-tuple-element.22), calls=%async_computation.1 | async-start | bytes 262144 | tf_op jit(solution)/shard_map/all_to_all | solution.py:284
  30.7 1.8 %all-gather.2 = f32[32,128]{1,0:T(8,128)S(1)} all-gather(f32[16,128]{1,0:T(8,128)S(1)} %get-tuple-element.23), channel_id=4, replica_groups=mesh['sys'=32,'mode'=8,'rank'=2] {'rank'}, dimensions={0}, use_global_device_ids=true | all-gather | bytes 24576 | tf_op jit(solution)/shard_map/all_gather | solution.py:285
  32.5 2.6 %shard_map.91 = (f32[64,128]{1,0:T(8,128)S(1)}, f32[64,1024]{1,0:T(8,128)S(1)}, bf16[256,1024]{1,0:T(8,128)(2,1)S(1)}) custom-call(f32[2,16,128]{2,1,0:T(8,128)S(1)} %bitcast.69, bf16[1024,64]{1,0:T(8,128)(2,1)S(1)} %bitcast.64), custom_call_target="tpu_custom_call" | custom-call | flops 4294967296 | bytes 1048576 | tf_op jit(solution)/shard_map/pallas_call | solution.py:27
  35.1 1.8 %all-to-all-done.1.recv_ref = f32[16,16,128]{2,1,0:T(8,128)S(1)} async-done(((f32[16,16,128]{2,1,0:T(8,128)}), f32[16,16,128]{2,1,0:T(8,128)S(1)}, u32[]{:S(2)}, u32[]{:S(2)}) %all-to-all-start.1) | async-done | bytes 131104 | tf_op jit(solution)/shard_map/all_to_all | solution.py:284
  36.9 1.8 %shard_map.92 = (f32[1024,80]{1,0:T(8,128)}, f32[80,80]{1,0:T(8,128)}) custom-call(f32[16,16,128]{2,1,0:T(8,128)S(1)} %all-to-all-done.1.recv_ref, f32[64,128]{1,0:T(8,128)S(1)} %get-tuple-element.24.both_ref, f32[64,1024]{1,0:T(8,128)S(1)} %get-tuple-element.25.ortho_ref, bf16[256,1024]{1,0:T(8,128)(2,1)S(1)} %get-tuple-element.26.parts_ref, ...), custom_call_target="tpu_custom_call" | custom-call | flops 67108864 | bytes 1048576 | tf_op jit(solution)/shard_map/pallas_call | solution.py:27
  (2 shorter events, 0.0 us)
Async XLA Ops:
  0.6 10.7 %copy-start = (bf16[8,128,32,8]{1,3,2,0:T(8,128)(2,1)S(1)}, bf16[8,128,32,8]{1,3,2,0:T(8,128)(2,1)}, u32[]{:S(2)}) copy-start(bf16[8,128,32,8]{1,3,2,0:T(8,128)(2,1)} %param.8) | copy-start | bytes 1572868
  0.6 9.8 %copy-start.5 = (bf16[16,16]{1,0:T(8,128)(2,1)S(1)}, bf16[16,16]{1,0:T(8,128)(2,1)}, u32[]{:S(2)}) copy-start(bf16[16,16]{1,0:T(8,128)(2,1)} %rhs_right_ref.1) | copy-start | bytes 1540
  0.7 9.8 %copy-start.2 = (bf16[16,32,16]{1,2,0:T(8,128)(2,1)S(1)}, bf16[16,32,16]{1,2,0:T(8,128)(2,1)}, u32[]{:S(2)}) copy-start(bf16[16,32,16]{1,2,0:T(8,128)(2,1)} %param.12) | copy-start | bytes 49156
  0.7 9.8 %copy-start.4 = (bf16[32,16]{0,1:T(8,128)(2,1)S(1)}, bf16[32,16]{0,1:T(8,128)(2,1)}, u32[]{:S(2)}) copy-start(bf16[32,16]{0,1:T(8,128)(2,1)} %param.11) | copy-start | bytes 3076
  0.7 9.8 %copy-start.3 = (bf16[64,8,16]{0,2,1:T(8,128)(2,1)S(1)}, bf16[64,8,16]{0,2,1:T(8,128)(2,1)}, u32[]{:S(2)}) copy-start(bf16[64,8,16]{0,2,1:T(8,128)(2,1)} %param.10) | copy-start | bytes 49156
  12.4 12.3 %copy-start.1 = (bf16[32,32,64]{2,1,0:T(8,128)(2,1)S(1)}, bf16[32,32,64]{2,1,0:T(8,128)(2,1)}, u32[]{:S(2)}) copy-start(bf16[32,32,64]{2,1,0:T(8,128)(2,1)} %param.7) | copy-start | bytes 393220
  25.9 11.0 %all-to-all-start.1 = ((f32[16,16,128]{2,1,0:T(8,128)}), f32[16,16,128]{2,1,0:T(8,128)S(1)}, u32[]{:S(2)}, u32[]{:S(2)}) async-start(f32[16,16,128]{2,1,0:T(8,128)} %get-tuple-element.22), calls=%async_computation.1 | async-start | bytes 262144 | tf_op jit(solution)/shard_map/all_to_all | solution.py:284

commit v6 on v5

--- a/solution.py
+++ b/solution.py
@@ -14,7 +14,7 @@
 RZ = 16
 RA = 8
 HALF = 32
-PITCH = 33
+PITCH = 36
 ROWS = 1024
 NT = (((1,), (1,)), ((), ()))
 TN = (((0,), (0,)), ((), ()))

time: 38.9 us -> 38.9 us (level)
  no operation moved by 1% of the time
where the time goes in v6:
time: 38.9 us; the launch traced here: 38.7 us
  blocking collectives  22.5 us (58%)
  Pallas kernels  7.68 us (20%)
  starting transfers between devices  4.8 us (12%)
  waiting for transfers between devices  1.82 us (5%)
  matrix products  1.1 us (3%)
  between operations  0.74 us (2%)
    all_to_all x1, blocking collectives, per_device(): recv = lax.all_to_all(send, 'mode', split_axis=0, concat_axis=0, tiled=True)  9.93 us
    all_gather x1, blocking collectives, per_device(): both = lax.all_gather(own, 'rank', axis=0)  8.74 us
    pallas_call x7, Pallas kernels, call(): pl.pallas_call(body, out_shape=outs, in_specs=in_specs or [VMEM] * len(ar...  7.68 us
    all_to_all x1, starting transfers between devices, per_device(): lax.all_to_all(send, ('mode', 'rank'), split_axis=0, concat_axis=0, tiled...  4.8 us
    all_gather x1, blocking collectives, per_device(): everyone = lax.all_gather(give, 'rank', axis=0)  2.01 us
    all_to_all x1, waiting for transfers between devices, per_device(): lax.all_to_all(send, ('mode', 'rank'), split_axis=0, concat_axis=0, tiled...  1.82 us
    all_gather x1, blocking collectives, per_device(): gram = lax.all_gather(gram, 'rank', axis=0)  1.81 us
    dot_general x1, matrix products, per_device(): jnp.einsum('cxa,cxib->aib', left, applied, preferred_element_type=F32)  1.1 us
  transfers between devices with their start and end apart: 1, of which 1 were waited for; matrix products, arithmetic and copies ran while one was open for 0% of the time, Pallas kernels for 7%

profile of v6, /device:TPU:1, one launch (start us, length us, event | category | flops | bytes accessed | tf_op | source)
XLA Modules:
  0.0 38.7 jit_solution(17493153244469517140)
XLA Ops:
  0.6 0.0 copy-start
  0.6 0.0 copy-start.5
  0.7 0.0 copy-start.2
  0.7 0.0 copy-start.4
  0.7 0.0 copy-start.3
  0.7 1.0 %shard_map.86 = bf16[1280,64]{1,0:T(8,128)(2,1)S(1)} custom-call(bf16[1024,64]{1,0:T(8,128)(2,1)} %bitcast.62, bf16[256,64]{1,0:T(8,128)(2,1)} %bitcast.71), custom_call_target="tpu_custom_call" | custom-call | bytes 1048576 | tf_op jit(solution)/shard_map/pallas_call | solution.py:27
  1.7 8.7 %all-gather = bf16[2560,64]{1,0:T(8,128)(2,1)S(1)} all-gather(bf16[1280,64]{1,0:T(8,128)(2,1)S(1)} %shard_map.86), channel_id=2, replica_groups=mesh['sys'=32,'mode'=8,'rank'=2] {'rank'}, dimensions={0}, use_global_device_ids=true | all-gather | bytes 491520 | tf_op jit(solution)/shard_map/all_gather | solution.py:235
  10.5 0.0 copy-done.5
  10.5 0.0 copy-done.2
  10.5 0.0 copy-done.4
  10.5 0.0 copy-done.3
  10.5 0.8 %shard_map.87 = (bf16[32,128,64]{2,1,0:T(8,128)(2,1)S(1)}, bf16[8,64,64]{2,1,0:T(8,128)(2,1)S(1)}, bf16[32,128]{1,0:T(8,128)(2,1)S(1)}, f32[128,128]{1,0:T(8,128)S(1)}) custom-call(s32[1]{0:T(128)} %bitcast.rank_ref, bf16[2,1280,64]{2,1,0:T(8,128)(2,1)S(1)} %bitcast.61, bf16[128,64]{1,0:T(8,128)(2,1)S(1)} %bitcast.68, bf16[16,32]{1,0:T(8,128)(2,1)S(1)} %bitcast.70, ...), custom_call_target="tpu_custom_call" | custom-call | flops 67108864 | bytes 1048576 | tf_op jit(solution)/shard_map/pallas_call | solution.py:27
  11.3 1.1 %fusion.8.part_ref = bf16[16,64,128]{2,1,0:T(8,128)(2,1)S(1)} fusion(bf16[64,32,8,16,1]{0,3,2,1,4:T(8,128)(2,1)S(1)} %bitcast.66, bf16[8,128,32,8]{1,3,2,0:T(8,128)(2,1)S(1)} %copy-done, bf16[8,64,64]{2,1,0:T(8,128)(2,1)S(1)} %get-tuple-element.16), kind=kOutput, calls=%fused_computation.5 | convolution fusion | flops 672268288 | bytes 1376256 | tf_op jit(solution)/shard_map/cxa,cxib->aib/dot_general | solution.py:260
  12.4 0.0 copy-start.1
  12.4 0.3 shard_map.88
  12.7 2.0 %all-gather.1 = bf16[8,128,128]{2,1,0:T(8,128)(2,1)S(1)} all-gather(bf16[4,128,128]{2,1,0:T(8,128)(2,1)S(1)} %get-tuple-element.19), channel_id=3, replica_groups=mesh['sys'=32,'mode'=8,'rank'=2] {'rank'}, dimensions={0}, use_global_device_ids=true | all-gather | bytes 393216 | tf_op jit(solution)/shard_map/all_gather | solution.py:264
  14.7 9.9 %all_to_all.10.recv_ref = bf16[8,160,128]{2,1,0:T(8,128)(2,1)S(1)} all-to-all(bf16[8,160,128]{2,1,0:T(8,128)(2,1)S(1)} %shard_map.89), channel_id=1, replica_groups=mesh['sys'=32,'mode'=8,'rank'=2] {'mode'}, dimensions={0} | all-to-all | bytes 655360 | tf_op jit(solution)/shard_map/all_to_all | solution.py:274
  24.7 0.0 copy-done.1
  24.7 1.2 %shard_map.90 = (f32[16,1024]{1,0:T(8,128)S(1)}, f32[16,16,128]{2,1,0:T(8,128)}, f32[16,128]{1,0:T(8,128)S(1)}) custom-call(bf16[8,160,128]{2,1,0:T(8,128)(2,1)S(1)} %all_to_all.10.recv_ref, f32[128,128]{1,0:T(8,128)S(1)} %get-tuple-element.21.rhs_ref, bf16[1024,64]{1,0:T(8,128)(2,1)S(1)} %bitcast.63), custom_call_target="tpu_custom_call" | custom-call | flops 16777216 | bytes 1048576 | tf_op jit(solution)/shard_map/pallas_call | solution.py:27
  25.9 4.8 %all-to-all-start.1 = ((f32[16,16,128]{2,1,0:T(8,128)}), f32[16,16,128]{2,1,0:T(8,128)S(1)}, u32[]{:S(2)}, u32[]{:S(2)}) async-start(f32[16,16,128]{2,1,0:T(8,128)} %get-tuple-element.22), calls=%async_computation.1 | async-start | bytes 262144 | tf_op jit(solution)/shard_map/all_to_all | solution.py:284
  30.7 1.8 %all-gather.2 = f32[32,128]{1,0:T(8,128)S(1)} all-gather(f32[16,128]{1,0:T(8,128)S(1)} %get-tuple-element.23), channel_id=4, replica_groups=mesh['sys'=32,'mode'=8,'rank'=2] {'rank'}, dimensions={0}, use_global_device_ids=true | all-gather | bytes 24576 | tf_op jit(solution)/shard_map/all_gather | solution.py:285
  32.5 2.6 %shard_map.91 = (f32[64,128]{1,0:T(8,128)S(1)}, f32[64,1024]{1,0:T(8,128)S(1)}, bf16[256,1024]{1,0:T(8,128)(2,1)S(1)}) custom-call(f32[2,16,128]{2,1,0:T(8,128)S(1)} %bitcast.69, bf16[1024,64]{1,0:T(8,128)(2,1)S(1)} %bitcast.64), custom_call_target="tpu_custom_call" | custom-call | flops 4294967296 | bytes 1048576 | tf_op jit(solution)/shard_map/pallas_call | solution.py:27
  35.0 1.8 %all-to-all-done.1.recv_ref = f32[16,16,128]{2,1,0:T(8,128)S(1)} async-done(((f32[16,16,128]{2,1,0:T(8,128)}), f32[16,16,128]{2,1,0:T(8,128)S(1)}, u32[]{:S(2)}, u32[]{:S(2)}) %all-to-all-start.1) | async-done | bytes 131104 | tf_op jit(solution)/shard_map/all_to_all | solution.py:284
  36.9 1.8 %shard_map.92 = (f32[1024,80]{1,0:T(8,128)}, f32[80,80]{1,0:T(8,128)}) custom-call(f32[16,16,128]{2,1,0:T(8,128)S(1)} %all-to-all-done.1.recv_ref, f32[64,128]{1,0:T(8,128)S(1)} %get-tuple-element.24.both_ref, f32[64,1024]{1,0:T(8,128)S(1)} %get-tuple-element.25.ortho_ref, bf16[256,1024]{1,0:T(8,128)(2,1)S(1)} %get-tuple-element.26.parts_ref, ...), custom_call_target="tpu_custom_call" | custom-call | flops 67108864 | bytes 1048576 | tf_op jit(solution)/shard_map/pallas_call | solution.py:27
  (2 shorter events, 0.0 us)
Async XLA Ops:
  0.6 10.6 %copy-start = (bf16[8,128,32,8]{1,3,2,0:T(8,128)(2,1)S(1)}, bf16[8,128,32,8]{1,3,2,0:T(8,128)(2,1)}, u32[]{:S(2)}) copy-start(bf16[8,128,32,8]{1,3,2,0:T(8,128)(2,1)} %param.8) | copy-start | bytes 1572868
  0.6 9.8 %copy-start.5 = (bf16[16,16]{1,0:T(8,128)(2,1)S(1)}, bf16[16,16]{1,0:T(8,128)(2,1)}, u32[]{:S(2)}) copy-start(bf16[16,16]{1,0:T(8,128)(2,1)} %rhs_right_ref.1) | copy-start | bytes 1540
  0.7 9.8 %copy-start.2 = (bf16[16,32,16]{1,2,0:T(8,128)(2,1)S(1)}, bf16[16,32,16]{1,2,0:T(8,128)(2,1)}, u32[]{:S(2)}) copy-start(bf16[16,32,16]{1,2,0:T(8,128)(2,1)} %param.12) | copy-start | bytes 49156
  0.7 9.8 %copy-start.4 = (bf16[32,16]{0,1:T(8,128)(2,1)S(1)}, bf16[32,16]{0,1:T(8,128)(2,1)}, u32[]{:S(2)}) copy-start(bf16[32,16]{0,1:T(8,128)(2,1)} %param.11) | copy-start | bytes 3076
  0.7 9.8 %copy-start.3 = (bf16[64,8,16]{0,2,1:T(8,128)(2,1)S(1)}, bf16[64,8,16]{0,2,1:T(8,128)(2,1)}, u32[]{:S(2)}) copy-start(bf16[64,8,16]{0,2,1:T(8,128)(2,1)} %param.10) | copy-start | bytes 49156
  12.4 12.3 %copy-start.1 = (bf16[32,32,64]{2,1,0:T(8,128)(2,1)S(1)}, bf16[32,32,64]{2,1,0:T(8,128)(2,1)}, u32[]{:S(2)}) copy-start(bf16[32,32,64]{2,1,0:T(8,128)(2,1)} %param.7) | copy-start | bytes 393220
  25.9 11.0 %all-to-all-start.1 = ((f32[16,16,128]{2,1,0:T(8,128)}), f32[16,16,128]{2,1,0:T(8,128)S(1)}, u32[]{:S(2)}, u32[]{:S(2)}) async-start(f32[16,16,128]{2,1,0:T(8,128)} %get-tuple-element.22), calls=%async_computation.1 | async-start | bytes 262144 | tf_op jit(solution)/shard_map/all_to_all | solution.py:284
